TPU v7x, 32 devices: a whole 2x2x4 slice. The times are simulated.
32 devices in a mesh: pitch: 4 (over x, core), span: 8 (over z, y).
Axes of the slice: x: 2, y: 2, z: 4, core: 2. Of those that a mesh axis runs over, the one named last changes fastest.
Arguments:
- residual: float32 [5, 4, 64, 1024], P(None, None, 'span', 'pitch'), may hold values from -0.6 to 0.6
- inverse_diagonal: float32 [5, 5, 4, 64, 1024], P(None, None, None, 'span', 'pitch'), may hold values from -0.1 to 1, as said below
- prior_increment: float32 [5, 4, 64, 1024], P(None, None, 'span', 'pitch'), may hold values from -3 to 3
- coupling: float32 [6, 5, 5], replicated, may hold values from -1 to 1
- characteristic: float32 [2, 2, 512, 5, 5], replicated, may hold values from -6 to 6
- cutoffs: int32 [2], replicated, may hold values from 128 to 512
Outputs:
- update: float32 [5, 4, 64, 1024], P(None, None, 'span', 'pitch')
Inputs may be any that keep to these rules, and one draw needn't show every extreme that they name: `inverse_diagonal`: each cell's block is dominated by its diagonal; the sweeps' recurrences are stable.
All inputs are finite; a program needn't handle non-finite values.
Results may differ from a plain program's by a relative error of at most 0.0003.
Values sent between devices are 32-bit elements; how exact they have to be, the bound alone decides.
No kernel may reach another device: no remote copies, remote signals or barrier semaphores. Data moves between devices by JAX's collectives and lax.ppermute only.
A program may use at most 64 MiB of HBM per device.

v0:
```python
import functools

import jax
import jax.numpy as jnp
import ml_dtypes
import numpy as np
from jax import lax
from jax.experimental import pallas as pl
from jax.experimental.pallas import tpu as pltpu
from jax.sharding import PartitionSpec as P


LANES = 128
HALF = 64
VMEM = pl.BlockSpec(memory_space=pltpu.VMEM)
SMEM = pl.BlockSpec(memory_space=pltpu.SMEM)
HBM = pl.BlockSpec(memory_space=pltpu.HBM)
ANY = pl.BlockSpec(memory_space=pl.ANY)
PARTS = 1
F32 = jnp.float32
BF16 = jnp.bfloat16


def call(kernel, outs, ins, specs, scratch=(), flops=1_000_000):
    moved = 4 * sum(int(np.prod(a.shape)) for a in ins)
    ins = [
        pltpu.with_memory_space_constraint(a, pltpu.HBM) if spec is HBM else a
        for a, spec in zip(ins, specs)
    ]
    return kernel_call(kernel, outs, ins, specs, scratch, flops, moved)


def kernel_call(kernel, outs, ins, specs, scratch, flops, moved):
    return pl.pallas_call(
        kernel,
        out_shape=[
            jax.ShapeDtypeStruct(*s) if isinstance(s[0], tuple) else jax.ShapeDtypeStruct(s, F32)
            for s in outs
        ],
        in_specs=list(specs),
        out_specs=[VMEM] * len(outs),
        scratch_shapes=list(scratch),
        cost_estimate=pl.CostEstimate(flops=flops, bytes_accessed=moved, transcendentals=0),
        compiler_params=pltpu.CompilerParams(vmem_limit_bytes=12 * 1024 * 1024),
    )(*ins)


def total(terms):
    result = terms[0]
    for term in terms[1:]:
        result = result + term
    return result


def matvec(get, vector):
    size = len(vector)
    return [total([get(i, j) * vector[j] for j in range(size)]) for i in range(size)]


def plus(a, b):
    return [x + y for x, y in zip(a, b)]


def split(x):
    high = x.astype(BF16)
    return high, (x - high.astype(F32)).astype(BF16)


def splat(coupling, which, i, j, shape):
    return jnp.broadcast_to(coupling[i, which : which + 1, j : j + 1], shape)


class Sizes:
    def __init__(self, residual, characteristic, pitch):
        self.v, self.axial, self.rows, self.width = residual.shape
        self.tiles = self.width // LANES
        self.block = self.tiles * self.rows
        self.cells = self.axial * self.tiles
        self.n = pitch
        self.points = pitch * self.width
        self.harmonics = characteristic.shape[2]
        self.per = self.harmonics // pitch
        self.planes = 2 * self.v * self.block
        self.vv = self.v * self.v
        self.parts = PARTS
        self.chunk = self.cells // self.parts


def to_tiles(array, sizes):
    lead = array.shape[:-3]
    array = array.reshape(lead + (sizes.axial, sizes.rows, sizes.tiles, LANES))
    array = jnp.swapaxes(array, -3, -2)
    return array.reshape((-1, sizes.axial * sizes.block, LANES))


def from_tiles(array, sizes):
    array = array.reshape((sizes.v, sizes.axial, sizes.tiles, sizes.rows, LANES))
    array = jnp.swapaxes(array, -3, -2)
    return array.reshape((sizes.v, sizes.axial, sizes.rows, sizes.width))


def payload_kernel(z, residual, prior, out, edges, sems):
    copies = []
    for q, a in enumerate((0, z.axial - 1)):
        for v in range(z.v):
            m = q * z.v + v
            copies.append(
                pltpu.make_async_copy(
                    residual.at[v, pl.ds(a * z.block, z.block), :],
                    out.at[pl.ds(m * z.block, z.block), :],
                    sems.at[m],
                )
            )
    copies.append(pltpu.make_async_copy(prior, edges, sems.at[2 * z.v]))
    for copy in copies[::-1]:
        copy.start()
    copies[-1].wait()
    lane = lax.broadcasted_iota(jnp.int32, (z.rows, LANES), 1)
    halo = jnp.zeros((z.rows, LANES), F32)
    for v in range(z.v):
        for a in range(z.axial):
            first = edges[v, pl.ds(a * z.block, z.rows), :][:, 0:1]
            last = edges[v, pl.ds((a + 1) * z.block - z.rows, z.rows), :][:, LANES - 1 :]
            halo = jnp.where(lane == v * z.axial + a, first, halo)
            halo = jnp.where(lane == HALF + v * z.axial + a, last, halo)
    out[pl.ds(z.planes, z.rows), :] = halo
    for copy in copies[:-1]:
        copy.wait()


def maps_kernel(z, diag_h, coupling_h, after, ops, *refs):
    del after
    outs, (maps, powers, diag, coupling, splats, sems) = refs[: z.parts], refs[z.parts :]
    span = range(z.v)
    vv = z.vv
    copies = [
        pltpu.make_async_copy(coupling_h, coupling, sems.at[0]),
        pltpu.make_async_copy(diag_h, diag, sems.at[1]),
    ]
    for copy in copies:
        copy.start()
    copies[0].wait()
    for which in range(2):
        for i in span:
            for j in span:
                splats[which * vv + i * z.v + j] = splat(
                    coupling, which, i, j, (z.cells, LANES)
                )
    copies[1].wait()

    def operators(r, _):
        for i in span:
            d = [diag[i * z.v + j, pl.ds(r, z.cells, stride=z.rows), :] for j in span]
            for k in span:
                for which in range(2):
                    ops[r, which * vv + i * z.v + k] = -total(
                        [d[j] * splats[which * vv + j * z.v + k] for j in span]
                    )
                ops[r, 2 * vv + i * z.v + k] = d[k]
        return 0

    lax.fori_loop(0, z.rows, operators, 0)

    for m in range(vv):
        powers[0, m] = ops[0, m]

    def forward(r, _):
        for k in span:
            column = [powers[r - 1, j * z.v + k] for j in span]
            new = matvec(lambda i, j: ops[r, i * z.v + j], column)
            for i in span:
                powers[r, i * z.v + k] = new[i]
        return 0

    lax.fori_loop(1, z.rows, forward, 0)
    top = z.rows - 1
    for m in range(vv):
        maps[m] = powers[top, m]
        maps[vv + m] = powers[top, m]
        maps[2 * vv + m] = ops[top, vv + m]

    def backward(step, _):
        r = top - step
        for k in span:
            for base in (vv, 2 * vv):
                column = [maps[base + j * z.v + k] for j in span]
                new = matvec(lambda i, j: ops[r, vv + i * z.v + j], column)
                for i in span:
                    value = new[i]
                    if base == vv:
                        value = value + powers[r, i * z.v + k]
                    maps[base + i * z.v + k] = value
        return 0

    lax.fori_loop(1, z.rows, backward, 0)
    for part in range(z.parts):
        for m in range(3 * vv):
            outs[part][m] = maps[m, pl.ds(part * z.chunk, z.chunk), :]


def prepare_kernel(z, *refs):
    residual_h, prior_h, char_h, high_h, low_h, coupling_h, cutoffs_h, after = refs[:8]
    source, spec, table_high, table_low, coupling, residual, prior, char, cutoffs, sems = refs[8:]
    del after
    span = range(z.v)
    vv = z.vv
    pairs = [
        (prior_h, prior),
        (residual_h, residual),
        (char_h, char),
        (high_h, table_high),
        (low_h, table_low),
        (coupling_h, coupling),
        (cutoffs_h, cutoffs),
    ]
    copies = [pltpu.make_async_copy(a, b, sems.at[k]) for k, (a, b) in enumerate(pairs)]
    for copy in copies:
        copy.start()

    for k in (5, 6, 0, 1):
        copies[k].wait()
    shape = (z.rows, LANES)
    factors = {
        (which, i, j): splat(coupling, which, i, j, shape)
        for which in range(2, 6)
        for i in span
        for j in span
    }

    def scalar(which, i, j):
        return factors[which, i, j]

    lane = lax.broadcasted_iota(jnp.int32, (z.rows, LANES), 1)

    def tile(ref, v, a, h):
        return ref[v, pl.ds(a * z.block + h * z.rows, z.rows), :]

    for a in range(z.axial):
        here = [[tile(prior, v, a, h) for h in range(z.tiles)] for v in span]
        up = [[pltpu.roll(x, 1, 1) for x in row] for row in here]
        down = [[pltpu.roll(x, LANES - 1, 1) for x in row] for row in here]
        for h in range(z.tiles):
            lower, upper = [], []
            for v in span:
                edge = up[v][h - 1] if h else jnp.zeros((z.rows, LANES), F32)
                lower.append(jnp.where(lane == 0, edge, up[v][h]))
                edge = down[v][h + 1] if h + 1 < z.tiles else jnp.zeros((z.rows, LANES), F32)
                upper.append(jnp.where(lane == LANES - 1, edge, down[v][h]))
            terms = [(2, lower), (3, upper)]
            if a > 0:
                terms.append((4, [tile(prior, v, a - 1, h) for v in span]))
            if a + 1 < z.axial:
                terms.append((5, [tile(prior, v, a + 1, h) for v in span]))
            for i in span:
                value = tile(residual, i, a, h)
                for which, field in terms:
                    value = value - total([field[j] * scalar(which, i, j) for j in span])
                source[i, pl.ds(a * z.block + h * z.rows, z.rows), :] = value

    k_of = lax.broadcasted_iota(jnp.int32, (z.harmonics, z.harmonics), 0)
    place = lax.broadcasted_iota(jnp.int32, (z.harmonics, z.harmonics), 1)
    wanted = (place % z.per) * z.n + place // z.per
    select = jnp.where(k_of == wanted, 1.0, 0.0).astype(BF16)
    copies[2].wait()
    for c in range(2):
        value = char[:, c, :]
        high, rest = split(value)
        rest = value - high.astype(F32)
        middle, low = split(rest)
        ordered = total(
            [jnp.dot(part, select, preferred_element_type=F32) for part in (high, middle, low)]
        )
        row = lax.broadcasted_iota(jnp.int32, ordered.shape, 0)
        place = lax.broadcasted_iota(jnp.int32, ordered.shape, 1)
        harmonic = (place % z.per) * z.n + place // z.per
        cutoff = jnp.where(row < vv, cutoffs[0], cutoffs[1])
        weight = jnp.where(harmonic == 0, 1.0, 2.0) / z.points
        spec[c] = ordered * jnp.where(harmonic < cutoff, weight, 0.0)
    copies[3].wait()
    copies[4].wait()


def spectral_kernel(z, *refs):
    blocks = refs[: z.n]
    table_high, table_low, spec, ops, source, coupling, driven, vectors, real, imag, total_source = (
        refs[z.n :]
    )
    span = range(z.v)
    vv = z.vv
    flat = 2 * z.v * z.rows

    def scalar(which, i, j):
        return coupling[i, which : which + 1, j : j + 1]

    def plane(ref):
        value = ref[pl.ds(0, z.planes), :].reshape(2 * z.v, z.tiles, z.rows, LANES)
        parts = [value[:, h].reshape(flat, LANES) for h in range(z.tiles)]
        return parts[0] if len(parts) == 1 else jnp.concatenate(parts, axis=1)

    x = [plane(ref) for ref in blocks]

    def combine(coefficients):
        terms = []
        for c, value in zip(coefficients, x):
            if abs(c) < 1e-12:
                continue
            if abs(c - 1) < 1e-12:
                terms.append(value)
            elif abs(c + 1) < 1e-12:
                terms.append(-value)
            else:
                terms.append(value * float(c))
        return total(terms) if terms else None

    def table(ref, s):
        return ref[:, pl.ds(2 * z.per * s, 2 * z.per)]

    turns = 2 * np.pi * np.arange(z.n) / z.n
    for s in range(z.n // 2 + 1):
        yr = combine(np.cos(turns * s))
        yi = combine(-np.sin(turns * s))
        highs, lows = zip(*[split(y) for y in (yr, yi) if y is not None])
        both = jnp.concatenate(highs + lows, axis=0)
        high = jnp.concatenate(highs, axis=0) if len(highs) > 1 else highs[0]
        rows = high.shape[0]
        for t in sorted({s, (z.n - s) % z.n}):
            first = jnp.dot(both, table(table_high, t), preferred_element_type=F32)
            second = jnp.dot(high, table(table_low, t), preferred_element_type=F32)
            y = first[:rows] + first[rows:] + second
            re, im = y[:flat, : z.per], -y[:flat, z.per :]
            if yi is not None:
                sign = 1.0 if t == s else -1.0
                re = re + sign * y[flat:, z.per :]
                im = im + sign * y[flat:, : z.per]
            real[:, pl.ds(z.per * t, z.per)] = re
            imag[:, pl.ds(z.per * t, z.per)] = im

    out_real, out_imag = [], []
    for q in range(2):
        rows = [pl.ds((q * z.v + j) * z.rows, z.rows) for j in span]
        re = [real[at, :] for at in rows]
        im = [imag[at, :] for at in rows]
        for i in span:
            base = (q * z.v + i) * z.v
            cr = [spec[0, pl.ds(base + j, 1), :] for j in span]
            ci = [spec[1, pl.ds(base + j, 1), :] for j in span]
            out_real.append(total([cr[j] * re[j] - ci[j] * im[j] for j in span]))
            out_imag.append(total([cr[j] * im[j] + ci[j] * re[j] for j in span]))
    cr = jnp.concatenate(out_real, axis=0)
    ci = -jnp.concatenate(out_imag, axis=0)
    parts = []
    for s in range(z.n):
        at = slice(s * z.per, (s + 1) * z.per)
        parts += [cr[:, at], ci[:, at]]
    high, low = split(jnp.concatenate(parts, axis=1))
    dims = (((1,), (1,)), ((), ()))
    both = jnp.concatenate([high, low], axis=0)
    first = lax.dot_general(both, table_high[...], dims, preferred_element_type=F32)
    second = lax.dot_general(high, table_low[...], dims, preferred_element_type=F32)
    correction = first[:flat] + first[flat:] + second

    lane = lax.broadcasted_iota(jnp.int32, (z.rows, LANES), 1)
    before = blocks[z.n - 1][pl.ds(z.planes, z.rows), :]
    after = blocks[1][pl.ds(z.planes, z.rows), :]
    for a in range(z.axial):
        lows = [before[:, HALF + v * z.axial + a : HALF + v * z.axial + a + 1] for v in span]
        highs = [after[:, v * z.axial + a : v * z.axial + a + 1] for v in span]
        for h in range(z.tiles):
            at = pl.ds(a * z.block + h * z.rows, z.rows)
            for i in span:
                value = source[i, at, :]
                if h == 0:
                    edge = total([lows[j] * scalar(2, i, j) for j in span])
                    value = value - jnp.where(lane == 0, edge, 0.0)
                if h == z.tiles - 1:
                    edge = total([highs[j] * scalar(3, i, j) for j in span])
                    value = value - jnp.where(lane == LANES - 1, edge, 0.0)
                for q, plane_a in enumerate((0, z.axial - 1)):
                    if a == plane_a:
                        first = (q * z.v + i) * z.rows
                        value = value + correction[
                            first : first + z.rows, h * LANES : (h + 1) * LANES
                        ]
                total_source[i, at, :] = value

    def drive(r, _):
        row = [total_source[j, pl.ds(r, z.cells, stride=z.rows), :] for j in span]
        new = matvec(lambda i, j: ops[r, 2 * vv + i * z.v + j], row)
        for i in span:
            driven[r, i] = new[i]
        return 0

    lax.fori_loop(0, z.rows, drive, 0)
    stars = [[driven[0, i] for i in span]]
    for r in range(1, z.rows):
        moved = matvec(lambda i, j: ops[r, i * z.v + j], stars[-1])
        stars.append([driven[r, i] + moved[i] for i in span])
    back = stars[-1]
    for r in range(z.rows - 2, -1, -1):
        back = plus(stars[r], matvec(lambda i, j: ops[r, vv + i * z.v + j], back))
    for i in span:
        vectors[i] = stars[-1][i]
        vectors[z.v + i] = back[i]


def place_pair(where, own, other, slots, lower, upper):
    def fill(a, b):
        for k, m in enumerate(lower):
            slots[k] = a[m]
        for k, m in enumerate(upper):
            slots[len(lower) + k] = b[m]

    @pl.when(where == 0)
    def _():
        fill(own, other)

    @pl.when(where != 0)
    def _():
        fill(other, own)


def merge_maps_kernel(z, level, last, device, own, other, out, slots):
    vv = z.vv
    every = list(range(3 * vv))
    place_pair((device[0] >> level) & 1, own, other, slots, every, every)
    span = range(z.v)

    def column(base, k):
        return [slots[base + j * z.v + k] for j in span]

    def apply(base, vector):
        return matvec(lambda i, j: slots[base + i * z.v + j], vector)

    up = 3 * vv
    for k in span:
        state = column(0, k)
        back = plus(column(vv, k), apply(2 * vv, apply(up + vv, state)))
        if last:
            for i in span:
                out[i * z.v + k] = back[i]
            continue
        state = apply(up, state)
        through = apply(2 * vv, column(up + 2 * vv, k))
        for i in span:
            out[i * z.v + k] = state[i]
            out[vv + i * z.v + k] = back[i]
            out[2 * vv + i * z.v + k] = through[i]


def merge_vectors_kernel(z, level, device, *refs):
    own_maps, other_maps = refs[: z.parts], refs[z.parts : 2 * z.parts]
    own, other, out, slots, vectors = refs[2 * z.parts :]
    vv = z.vv
    span = range(z.v)
    bit = (device[0] >> level) & 1
    every = list(range(2 * z.v))
    place_pair(bit, own, other, vectors, every, every)
    for part in range(z.parts):
        at = pl.ds(part * z.chunk, z.chunk)
        place_pair(
            bit, own_maps[part], other_maps[part], slots, range(2 * vv, 3 * vv), range(2 * vv)
        )

        def apply(base, vector):
            return matvec(lambda i, j: slots[base + i * z.v + j], vector)

        fa, ha, fb, hb = [[vectors[k * z.v + i, at, :] for i in span] for k in range(4)]
        state = plus(fb, apply(vv, fa))
        back = plus(ha, apply(0, plus(hb, apply(2 * vv, fa))))
        for i in span:
            out[i, at, :] = state[i]
            out[z.v + i, at, :] = back[i]


def final_kernel(z, levels, device, *refs):
    span = range(z.v)
    vv = z.vv
    refs = list(refs)

    def take(count):
        taken = refs[:count]
        del refs[:count]
        return taken

    inner_maps = [(take(z.parts), take(z.parts)) for _ in range(levels - 1)]
    outer = take(z.parts)
    vector_pairs = [take(2) for _ in range(levels)]
    ops, driven, out, slots, vectors, inside, stars = refs

    def load(base, at):
        return [inside[base + i, at, :] for i in span]

    for level in range(levels - 1, -1, -1):
        bit = (device[0] >> level) & 1
        own, other = vector_pairs[level]
        place_pair(bit, own, other, vectors, range(z.v), range(z.v, 2 * z.v))
        for part in range(z.parts):
            at = pl.ds(part * z.chunk, z.chunk)
            fa, hb = [[vectors[k * z.v + i, at, :] for i in span] for k in range(2)]
            if level == levels - 1:
                back = plus(hb, matvec(lambda i, j: outer[part][i * z.v + j], fa))
                zero = [jnp.zeros_like(value) for value in fa]
                xa, ya, xb, yb = zero, back, fa, zero
            else:
                own, other = inner_maps[level]
                place_pair(bit, own[part], other[part], slots, range(vv), range(vv, 3 * vv))

                def apply(base, vector):
                    return matvec(lambda i, j: slots[base + i * z.v + j], vector)

                xa, yb = load(0, at), load(z.v, at)
                xb = plus(fa, apply(0, xa))
                ya = plus(plus(hb, apply(vv, xb)), apply(2 * vv, yb))
            for i in span:
                inside[i, at, :] = jnp.where(bit == 0, xa[i], xb[i])
                inside[z.v + i, at, :] = jnp.where(bit == 0, ya[i], yb[i])

    x = [inside[i] for i in span]
    y = [inside[z.v + i] for i in span]
    for r in range(z.rows):
        x = plus([driven[r, i] for i in span], matvec(lambda i, j: ops[r, i * z.v + j], x))
        for i in span:
            stars[r, i] = x[i]
    for r in range(z.rows - 1, -1, -1):
        y = plus(
            [stars[r, i] for i in span], matvec(lambda i, j: ops[r, vv + i * z.v + j], y)
        )
        for i in span:
            out[i, pl.ds(r, z.cells, stride=z.rows), :] = y[i]


def trig_tables(z):
    q = np.arange(z.width)[:, None]
    k = (np.arange(z.n)[:, None] + z.n * np.arange(z.per)[None, :]).reshape(1, z.n, 1, z.per)
    angle = 2 * np.pi * ((q.reshape(-1, 1, 1, 1) * k) % z.points) / z.points
    values = np.concatenate([np.cos(angle), np.sin(angle)], axis=2).reshape(z.width, -1)
    high = values.astype(np.float32).astype(ml_dtypes.bfloat16)
    low = (values - high.astype(np.float64)).astype(np.float32).astype(ml_dtypes.bfloat16)
    return high, low


def exchange(value, span, level, both=True):
    pairs = [(d ^ (1 << level), d) for d in range(span) if both or not (d >> level) & 1]
    return lax.ppermute(value, "span", pairs)


def body(residual, inverse_diagonal, prior_increment, coupling, characteristic, cutoffs):
    pitch, span = lax.axis_size("pitch"), lax.axis_size("span")
    z = Sizes(residual, characteristic, pitch)
    vv = z.vv
    levels = span.bit_length() - 1
    residual_t = to_tiles(residual, z)
    prior_t = to_tiles(prior_increment, z)
    diag_t = to_tiles(inverse_diagonal, z)
    couple = jnp.transpose(coupling, (1, 0, 2))
    char = jnp.transpose(characteristic, (0, 3, 4, 1, 2)).reshape(-1, 2, z.harmonics)
    device = lax.axis_index("span").astype(jnp.int32).reshape(1)
    cell, part_cell = (z.cells, LANES), (z.chunk, LANES)
    field = (z.v, z.axial * z.block, LANES)
    scratch = pltpu.VMEM

    payload = call(
        functools.partial(payload_kernel, z),
        [(z.planes + z.rows, LANES)],
        (residual_t, prior_t),
        [HBM] * 2,
        [scratch(field, F32), pltpu.SemaphoreType.DMA((2 * z.v + 1,))],
    )[0]
    blocks = [payload]
    for j in range(1, pitch):
        pairs = [((e + j) % pitch, e) for e in range(pitch)]
        blocks.append(lax.ppermute(payload, "pitch", pairs))

    ops, *maps = call(
        functools.partial(maps_kernel, z),
        [(z.rows, 3 * vv) + cell] + [(3 * vv,) + part_cell] * z.parts,
        (diag_t, couple, payload),
        [HBM, HBM, ANY],
        [
            scratch((3 * vv,) + cell, F32),
            scratch((z.rows, vv) + cell, F32),
            scratch(diag_t.shape, F32),
            scratch(couple.shape, F32),
            scratch((2 * vv,) + cell, F32),
            pltpu.SemaphoreType.DMA((2,)),
        ],
        flops=10_000_000,
    )
    map_levels = []
    for level in range(levels):
        last = level == levels - 1
        others = []
        for value in maps:
            others.append(exchange(value, span, level, not last))
        map_levels.append((maps, others))
        if last:
            break
        count = vv if level == levels - 2 else 3 * vv
        maps = [
            call(
                functools.partial(merge_maps_kernel, z, level, level == levels - 2),
                [(count,) + part_cell],
                (device, mine, other),
                [SMEM, VMEM, VMEM],
                [scratch((6 * vv,) + part_cell, F32)],
            )[0]
            for mine, other in zip(maps, others)
        ]

    high, low = trig_tables(z)
    source, spec, high, low, couple = call(
        functools.partial(prepare_kernel, z),
        [field, (2, 2 * vv, z.harmonics), (high.shape, BF16), (low.shape, BF16), couple.shape],
        (
            residual_t,
            prior_t,
            char,
            jnp.asarray(high),
            jnp.asarray(low),
            couple,
            cutoffs,
            payload,
        ),
        [HBM] * 7 + [ANY],
        [
            scratch(field, F32),
            scratch(field, F32),
            scratch(char.shape, F32),
            pltpu.SMEM(cutoffs.shape, jnp.int32),
            pltpu.SemaphoreType.DMA((7,)),
        ],
        flops=5_000_000,
    )

    rows = 2 * z.v * z.rows
    driven, vectors = call(
        functools.partial(spectral_kernel, z),
        [(z.rows, z.v) + cell, (2 * z.v,) + cell],
        (*blocks, high, low, spec, ops, source, couple),
        [VMEM] * (z.n + 6),
        [
            scratch((rows, z.harmonics), F32),
            scratch((rows, z.harmonics), F32),
            scratch(field, F32),
        ],
        flops=10_000_000,
    )

    vector_levels = []
    for level in range(levels):
        other = exchange(vectors, span, level)
        vector_levels.append((vectors, other))
        if level + 1 < levels:
            mine, others = map_levels[level]
            vectors = call(
                functools.partial(merge_vectors_kernel, z, level),
                [(2 * z.v,) + cell],
                (device, *mine, *others, vectors, other),
                [SMEM] + [VMEM] * (2 * z.parts + 2),
                [scratch((3 * vv,) + part_cell, F32), scratch((4 * z.v,) + cell, F32)],
            )[0]

    arrays = []
    for mine, others in map_levels[:-1]:
        arrays += [*mine, *others]
    arrays += map_levels[-1][1]
    for pair in vector_levels:
        arrays += pair
    update = call(
        functools.partial(final_kernel, z, levels),
        [field],
        (device, *arrays, ops, driven),
        [SMEM] + [VMEM] * (len(arrays) + 2),
        [
            scratch((3 * vv,) + part_cell, F32),
            scratch((2 * z.v,) + cell, F32),
            scratch((2 * z.v,) + cell, F32),
            scratch((z.rows, z.v) + cell, F32),
        ],
        flops=2_000_000,
    )[0]
    return from_tiles(update, z)


def solution(mesh):
    in_specs = (
        P(None, None, "span", "pitch"),
        P(None, None, None, "span", "pitch"),
        P(None, None, "span", "pitch"),
        P(),
        P(),
        P(),
    )
    out_specs = P(None, None, "span", "pitch")
    return jax.shard_map(body, mesh=mesh, in_specs=in_specs, out_specs=out_specs, check_vma=False)
```

profile of v0, /device:TPU:0, one launch (start us, length us, event | category | flops | bytes accessed | tf_op | source)
XLA Modules:
  0.0 40.8 jit_solution(13523786238356032591)
XLA Ops:
  0.0 1.1 %shard_map.82.after.refs_7_.refs_0_ = f32[168,128]{1,0:T(8,128)S(1)} custom-call(f32[5,64,128]{2,1,0:T(8,128)} %bitcast.26, f32[5,64,128]{2,1,0:T(8,128)} %bitcast.28), custom_call_target="tpu_custom_call" | custom-call | flops 1000000 | bytes 327680 | tf_op jit(solution)/shard_map/pallas_call | solution.py:34
  1.1 2.7 %shard_map.83 = (f32[8,75,8,128]{3,2,1,0:T(8,128)S(1)}, f32[75,8,128]{2,1,0:T(8,128)S(1)}) custom-call(f32[25,64,128]{2,1,0:T(8,128)} %bitcast.25, f32[5,6,5]{2,1,0:T(8,128)} %bitcast.31, f32[168,128]{1,0:T(8,128)S(1)} %shard_map.82.after.refs_7_.refs_0_), custom_call_target="tpu_custom_call" | custom-call | flops 10000000 | bytes 905816 | tf_op jit(solution)/shard_map/pallas_call | solution.py:34
  3.9 3.1 %collective-permute-start = (f32[75,8,128]{2,1,0:T(8,128)S(1)}, f32[75,8,128]{2,1,0:T(8,128)S(1)}, u32[]{:S(2)}, u32[]{:S(2)}) collective-permute-start(f32[75,8,128]{2,1,0:T(8,128)S(1)} %get-tuple-element.14.own.refs_0_), channel_id=1, source_target_pairs={{1,0},{0,1},{3,2},{2,3},{5,4},{4,5},{7,6},{6,7},{9,8},{8,9},{11,10... | collective-permute-start | bytes 921608 | tf_op jit(solution)/shard_map/ppermute | solution.py:544
  7.0 7.3 %collective-permute-done.other.refs_1_ = f32[75,8,128]{2,1,0:T(8,128)S(1)} collective-permute-done((f32[75,8,128]{2,1,0:T(8,128)S(1)}, f32[75,8,128]{2,1,0:T(8,128)S(1)}, u32[]{:S(2)}, u32[]{:S(2)}) %collective-permute-start) | collective-permute-done | bytes 307232 | tf_op jit(solution)/shard_map/ppermute | solution.py:544
  14.2 0.2 shard_map.84.own.refs_0_.refs_2_
  14.4 1.9 %collective-permute-start.1 = (f32[75,8,128]{2,1,0:T(8,128)S(1)}, f32[75,8,128]{2,1,0:T(8,128)S(1)}, u32[]{:S(2)}, u32[]{:S(2)}) collective-permute-start(f32[75,8,128]{2,1,0:T(8,128)S(1)} %shard_map.84.own.refs_0_.refs_2_), channel_id=1, source_target_pairs={{2,0},{3,1},{0,2},{1,3},{6,4},{7,5},{4,6},{5,7},{10,8},{11,9},{8,1... | collective-permute-start | bytes 921608 | tf_op jit(solution)/shard_map/ppermute | solution.py:544
  16.3 0.0 collective-permute-start.3
  16.3 1.5 %collective-permute-start.4 = (f32[168,128]{1,0:T(8,128)S(1)}, f32[168,128]{1,0:T(8,128)S(1)}, u32[]{:S(2)}, u32[]{:S(2)}) collective-permute-start(f32[168,128]{1,0:T(8,128)S(1)} %shard_map.82.after.refs_7_.refs_0_), channel_id=1, source_target_pairs={{16,0},{24,8},{0,16},{8,24},{17,1},{25,9},{1,17},{9,25},{18,2},{26... | collective-permute-start | bytes 258056 | tf_op jit(solution)/shard_map/ppermute | solution.py:572
  17.8 0.2 collective-permute-start.5
  18.0 3.3 %shard_map.86 = (f32[5,64,128]{2,1,0:T(8,128)S(1)}, f32[2,50,512]{2,1,0:T(8,128)S(1)}, bf16[256,1024]{1,0:T(8,128)(2,1)S(1)}, bf16[256,1024]{1,0:T(8,128)(2,1)S(1)}, f32[5,6,5]{2,1,0:T(8,128)S(1)}) custom-call(f32[5,64,128]{2,1,0:T(8,128)} %bitcast.27, f32[5,64,128]{2,1,0:T(8,128)} %bitcast.29, f32[50,2,512]{2,1,0:T(2,128)} %bitcast.30, ...), custom_call_target="tpu_custom_call" | custom-call | flops 5000000 | bytes 2716256 | tf_op jit(solution)/shard_map/pallas_call | solution.py:34
  21.3 0.0 collective-permute-done.3.refs_1_
  21.3 1.6 %collective-permute-done.4.refs_2_ = f32[168,128]{1,0:T(8,128)S(1)} collective-permute-done((f32[168,128]{1,0:T(8,128)S(1)}, f32[168,128]{1,0:T(8,128)S(1)}, u32[]{:S(2)}, u32[]{:S(2)}) %collective-permute-start.4) | collective-permute-done | bytes 86048 | tf_op jit(solution)/shard_map/ppermute | solution.py:572
  22.9 0.1 collective-permute-done.5.refs_3_
  23.0 3.5 %shard_map.87 = (f32[8,5,8,128]{3,2,1,0:T(8,128)S(1)}, f32[10,8,128]{2,1,0:T(8,128)S(1)}) custom-call(f32[168,128]{1,0:T(8,128)S(1)} %shard_map.82.after.refs_7_.refs_0_, f32[168,128]{1,0:T(8,128)S(1)} %collective-permute-done.3.refs_1_, f32[168,128]{1,0:T(8,128)S(1)} %collective-permute-done.4.refs_2_, f32[168,128]{1,0:T(8,128)S(1)} %collective-permute-done.5.refs_3_, ...), custom_call_target="tpu_custom_call" | custom-call | flops 10000000 | bytes 5268056 | tf_op jit(solution)/shard_map/pallas_call | solution.py:34
  26.5 1.6 %collective-permute-start.6 = (f32[10,8,128]{2,1,0:T(8,128)S(1)}, f32[10,8,128]{2,1,0:T(8,128)S(1)}, u32[]{:S(2)}, u32[]{:S(2)}) collective-permute-start(f32[10,8,128]{2,1,0:T(8,128)S(1)} %get-tuple-element.21.refs_2_.refs_5_), channel_id=1, source_target_pairs={{1,0},{0,1},{3,2},{2,3},{5,4},{4,5},{7,6},{6,7},{9,8},{8,9},{11,10... | collective-permute-start | bytes 122888 | tf_op jit(solution)/shard_map/ppermute | solution.py:544
  28.0 0.0 collective-permute-done.1.other.refs_1_.refs_3_
  28.0 0.1 shard_map.85
  28.2 1.3 %collective-permute-start.2 = (f32[25,8,128]{2,1,0:T(8,128)S(1)}, f32[25,8,128]{2,1,0:T(8,128)S(1)}, u32[]{:S(2)}, u32[]{:S(2)}) collective-permute-start(f32[25,8,128]{2,1,0:T(8,128)S(1)} %shard_map.85), channel_id=1, source_target_pairs={{4,0},{5,1},{6,2},{7,3},{12,8},{13,9},{14,10},{15,11},{20,16},{21,... | collective-permute-start | bytes 307208 | tf_op jit(solution)/shard_map/ppermute | solution.py:544
  29.5 1.1 %collective-permute-done.6.refs_3_.refs_6_ = f32[10,8,128]{2,1,0:T(8,128)S(1)} collective-permute-done((f32[10,8,128]{2,1,0:T(8,128)S(1)}, f32[10,8,128]{2,1,0:T(8,128)S(1)}, u32[]{:S(2)}, u32[]{:S(2)}) %collective-permute-start.6) | collective-permute-done | bytes 40992 | tf_op jit(solution)/shard_map/ppermute | solution.py:544
  30.5 0.1 shard_map.88.refs_2_.refs_7_
  30.6 0.4 collective-permute-start.7
  31.0 3.7 %collective-permute-done.7.refs_3_.refs_8_ = f32[10,8,128]{2,1,0:T(8,128)S(1)} collective-permute-done((f32[10,8,128]{2,1,0:T(8,128)S(1)}, f32[10,8,128]{2,1,0:T(8,128)S(1)}, u32[]{:S(2)}, u32[]{:S(2)}) %collective-permute-start.7) | collective-permute-done | bytes 40992 | tf_op jit(solution)/shard_map/ppermute | solution.py:544
  34.7 0.1 shard_map.89.refs_9_
  34.7 2.6 %collective-permute-start.8 = (f32[10,8,128]{2,1,0:T(8,128)S(1)}, f32[10,8,128]{2,1,0:T(8,128)S(1)}, u32[]{:S(2)}, u32[]{:S(2)}) collective-permute-start(f32[10,8,128]{2,1,0:T(8,128)S(1)} %shard_map.89.refs_9_), channel_id=1, source_target_pairs={{4,0},{5,1},{6,2},{7,3},{0,4},{1,5},{2,6},{3,7},{12,8},{13,9},{14,... | collective-permute-start | bytes 122888 | tf_op jit(solution)/shard_map/ppermute | solution.py:544
  37.4 2.5 %collective-permute-done.8.refs_10_ = f32[10,8,128]{2,1,0:T(8,128)S(1)} collective-permute-done((f32[10,8,128]{2,1,0:T(8,128)S(1)}, f32[10,8,128]{2,1,0:T(8,128)S(1)}, u32[]{:S(2)}, u32[]{:S(2)}) %collective-permute-start.8) | collective-permute-done | bytes 40992 | tf_op jit(solution)/shard_map/ppermute | solution.py:544
  39.9 0.0 collective-permute-done.2.refs_4_
  39.9 0.9 %shard_map.90 = f32[5,64,128]{2,1,0:T(8,128)} custom-call(s32[1]{0:T(128)} %bitcast.device, f32[75,8,128]{2,1,0:T(8,128)S(1)} %get-tuple-element.14.own.refs_0_, f32[75,8,128]{2,1,0:T(8,128)S(1)} %collective-permute-done.other.refs_1_, f32[75,8,128]{2,1,0:T(8,128)S(1)} %shard_map.84.own.refs_0_.refs_2_, ...), custom_call_target="tpu_custom_call" | custom-call | flops 2000000 | bytes 4198404 | tf_op jit(solution)/shard_map/pallas_call | solution.py:34
Async XLA Ops:
  3.9 10.3 %collective-permute-start = (f32[75,8,128]{2,1,0:T(8,128)S(1)}, f32[75,8,128]{2,1,0:T(8,128)S(1)}, u32[]{:S(2)}, u32[]{:S(2)}) collective-permute-start(f32[75,8,128]{2,1,0:T(8,128)S(1)} %get-tuple-element.14.own.refs_0_), channel_id=1, source_target_pairs={{1,0},{0,1},{3,2},{2,3},{5,4},{4,5},{7,6},{6,7},{9,8},{8,9},{11,10... | collective-permute-start | bytes 921608 | tf_op jit(solution)/shard_map/ppermute | solution.py:544
  14.4 13.6 %collective-permute-start.1 = (f32[75,8,128]{2,1,0:T(8,128)S(1)}, f32[75,8,128]{2,1,0:T(8,128)S(1)}, u32[]{:S(2)}, u32[]{:S(2)}) collective-permute-start(f32[75,8,128]{2,1,0:T(8,128)S(1)} %shard_map.84.own.refs_0_.refs_2_), channel_id=1, source_target_pairs={{2,0},{3,1},{0,2},{1,3},{6,4},{7,5},{4,6},{5,7},{10,8},{11,9},{8,1... | collective-permute-start | bytes 921608 | tf_op jit(solution)/shard_map/ppermute | solution.py:544
  16.3 5.1 %collective-permute-start.3 = (f32[168,128]{1,0:T(8,128)S(1)}, f32[168,128]{1,0:T(8,128)S(1)}, u32[]{:S(2)}, u32[]{:S(2)}) collective-permute-start(f32[168,128]{1,0:T(8,128)S(1)} %shard_map.82.after.refs_7_.refs_0_), channel_id=1, source_target_pairs={{8,0},{16,8},{24,16},{0,24},{9,1},{17,9},{25,17},{1,25},{10,2},{18... | collective-permute-start | bytes 258056 | tf_op jit(solution)/shard_map/ppermute | solution.py:572
  16.3 6.6 %collective-permute-start.4 = (f32[168,128]{1,0:T(8,128)S(1)}, f32[168,128]{1,0:T(8,128)S(1)}, u32[]{:S(2)}, u32[]{:S(2)}) collective-permute-start(f32[168,128]{1,0:T(8,128)S(1)} %shard_map.82.after.refs_7_.refs_0_), channel_id=1, source_target_pairs={{16,0},{24,8},{0,16},{8,24},{17,1},{25,9},{1,17},{9,25},{18,2},{26... | collective-permute-start | bytes 258056 | tf_op jit(solution)/shard_map/ppermute | solution.py:572
  17.8 5.2 %collective-permute-start.5 = (f32[168,128]{1,0:T(8,128)S(1)}, f32[168,128]{1,0:T(8,128)S(1)}, u32[]{:S(2)}, u32[]{:S(2)}) collective-permute-start(f32[168,128]{1,0:T(8,128)S(1)} %shard_map.82.after.refs_7_.refs_0_), channel_id=1, source_target_pairs={{24,0},{0,8},{8,16},{16,24},{25,1},{1,9},{9,17},{17,25},{26,2},{2,... | collective-permute-start | bytes 258056 | tf_op jit(solution)/shard_map/ppermute | solution.py:572
  26.5 4.1 %collective-permute-start.6 = (f32[10,8,128]{2,1,0:T(8,128)S(1)}, f32[10,8,128]{2,1,0:T(8,128)S(1)}, u32[]{:S(2)}, u32[]{:S(2)}) collective-permute-start(f32[10,8,128]{2,1,0:T(8,128)S(1)} %get-tuple-element.21.refs_2_.refs_5_), channel_id=1, source_target_pairs={{1,0},{0,1},{3,2},{2,3},{5,4},{4,5},{7,6},{6,7},{9,8},{8,9},{11,10... | collective-permute-start | bytes 122888 | tf_op jit(solution)/shard_map/ppermute | solution.py:544
  28.2 11.7 %collective-permute-start.2 = (f32[25,8,128]{2,1,0:T(8,128)S(1)}, f32[25,8,128]{2,1,0:T(8,128)S(1)}, u32[]{:S(2)}, u32[]{:S(2)}) collective-permute-start(f32[25,8,128]{2,1,0:T(8,128)S(1)} %shard_map.85), channel_id=1, source_target_pairs={{4,0},{5,1},{6,2},{7,3},{12,8},{13,9},{14,10},{15,11},{20,16},{21,... | collective-permute-start | bytes 307208 | tf_op jit(solution)/shard_map/ppermute | solution.py:544
  30.6 4.1 %collective-permute-start.7 = (f32[10,8,128]{2,1,0:T(8,128)S(1)}, f32[10,8,128]{2,1,0:T(8,128)S(1)}, u32[]{:S(2)}, u32[]{:S(2)}) collective-permute-start(f32[10,8,128]{2,1,0:T(8,128)S(1)} %shard_map.88.refs_2_.refs_7_), channel_id=1, source_target_pairs={{2,0},{3,1},{0,2},{1,3},{6,4},{7,5},{4,6},{5,7},{10,8},{11,9},{8,1... | collective-permute-start | bytes 122888 | tf_op jit(solution)/shard_map/ppermute | solution.py:544
  34.7 5.1 %collective-permute-start.8 = (f32[10,8,128]{2,1,0:T(8,128)S(1)}, f32[10,8,128]{2,1,0:T(8,128)S(1)}, u32[]{:S(2)}, u32[]{:S(2)}) collective-permute-start(f32[10,8,128]{2,1,0:T(8,128)S(1)} %shard_map.89.refs_9_), channel_id=1, source_target_pairs={{4,0},{5,1},{6,2},{7,3},{0,4},{1,5},{2,6},{3,7},{12,8},{13,9},{14,... | collective-permute-start | bytes 122888 | tf_op jit(solution)/shard_map/ppermute | solution.py:544
where the time goes:
time: 41 us; the launch traced here: 40.8 us
  waiting for transfers between devices  16.2 us (40%)
  starting transfers between devices  12.5 us (30%)
  Pallas kernels  12 us (29%)
    ppermute x6, waiting for transfers between devices, exchange(): return lax.ppermute(value, 'span', pairs)  14.6 us
    pallas_call x9, Pallas kernels, kernel_call(): pl.pallas_call(kernel, out_shape=[jax.ShapeDtypeStruct(*s) if isinstance(...  12 us
    ppermute x6, starting transfers between devices, exchange(): return lax.ppermute(value, 'span', pairs)  10.8 us
    ppermute x3, starting transfers between devices, body(): blocks.append(lax.ppermute(payload, 'pitch', pairs))  1.72 us
    ppermute x3, waiting for transfers between devices, body(): blocks.append(lax.ppermute(payload, 'pitch', pairs))  1.66 us
  transfers between devices with their start and end apart: 9, of which 6 were waited for; matrix products, arithmetic and copies ran while one was open for 0% of the time, Pallas kernels for 17%

commit v1 on v0

--- a/solution.py
+++ b/solution.py
@@ -17,6 +17,7 @@
 HBM = pl.BlockSpec(memory_space=pltpu.HBM)
 ANY = pl.BlockSpec(memory_space=pl.ANY)
 PARTS = 1
+MIRRORED = True
 F32 = jnp.float32
 BF16 = jnp.bfloat16
 
@@ -46,10 +47,11 @@
 
 
 def total(terms):
-    result = terms[0]
-    for term in terms[1:]:
-        result = result + term
-    return result
+    terms = list(terms)
+    while len(terms) > 1:
+        paired = [a + b for a, b in zip(terms[::2], terms[1::2])]
+        terms = paired + terms[2 * len(paired) :]
+    return terms[0]
 
 
 def matvec(get, vector):
@@ -99,53 +101,42 @@
     return array.reshape((sizes.v, sizes.axial, sizes.rows, sizes.width))
 
 
-def payload_kernel(z, residual, prior, out, edges, sems):
-    copies = []
-    for q, a in enumerate((0, z.axial - 1)):
-        for v in range(z.v):
-            m = q * z.v + v
-            copies.append(
-                pltpu.make_async_copy(
-                    residual.at[v, pl.ds(a * z.block, z.block), :],
-                    out.at[pl.ds(m * z.block, z.block), :],
-                    sems.at[m],
-                )
-            )
-    copies.append(pltpu.make_async_copy(prior, edges, sems.at[2 * z.v]))
-    for copy in copies[::-1]:
-        copy.start()
-    copies[-1].wait()
-    lane = lax.broadcasted_iota(jnp.int32, (z.rows, LANES), 1)
-    halo = jnp.zeros((z.rows, LANES), F32)
-    for v in range(z.v):
-        for a in range(z.axial):
-            first = edges[v, pl.ds(a * z.block, z.rows), :][:, 0:1]
-            last = edges[v, pl.ds((a + 1) * z.block - z.rows, z.rows), :][:, LANES - 1 :]
-            halo = jnp.where(lane == v * z.axial + a, first, halo)
-            halo = jnp.where(lane == HALF + v * z.axial + a, last, halo)
-    out[pl.ds(z.planes, z.rows), :] = halo
-    for copy in copies[:-1]:
-        copy.wait()
-
-
-def maps_kernel(z, diag_h, coupling_h, after, ops, *refs):
-    del after
-    outs, (maps, powers, diag, coupling, splats, sems) = refs[: z.parts], refs[z.parts :]
-    span = range(z.v)
-    vv = z.vv
+def opening_kernel(z, *refs):
+    ins, refs = refs[:4], refs[4:]
+    residual, prior, coupling, payload, ops = refs[:5]
+    outs, (maps, powers, diag, splats, sems) = refs[5 : 5 + z.parts], refs[5 + z.parts :]
+    held = [coupling, diag, prior, residual]
     copies = [
-        pltpu.make_async_copy(coupling_h, coupling, sems.at[0]),
-        pltpu.make_async_copy(diag_h, diag, sems.at[1]),
+        pltpu.make_async_copy(a, b, sems.at[k]) for k, (a, b) in enumerate(zip(ins, held))
     ]
     for copy in copies:
         copy.start()
+    span = range(z.v)
+    vv = z.vv
+
     copies[0].wait()
     for which in range(2):
         for i in span:
             for j in span:
-                splats[which * vv + i * z.v + j] = splat(
+                splats[which * vv + i * z.v + j] = -splat(
                     coupling, which, i, j, (z.cells, LANES)
                 )
+    copies[2].wait()
+    lane = lax.broadcasted_iota(jnp.int32, (z.rows, LANES), 1)
+    halo = jnp.zeros((z.rows, LANES), F32)
+    for v in span:
+        for a in range(z.axial):
+            first = prior[v, pl.ds(a * z.block, z.rows), :][:, 0:1]
+            last = prior[v, pl.ds((a + 1) * z.block - z.rows, z.rows), :][:, LANES - 1 :]
+            halo = jnp.where(lane == v * z.axial + a, first, halo)
+            halo = jnp.where(lane == HALF + v * z.axial + a, last, halo)
+    payload[pl.ds(z.planes, z.rows), :] = halo
+    copies[3].wait()
+    for q, a in enumerate((0, z.axial - 1)):
+        for v in span:
+            payload[pl.ds((q * z.v + v) * z.block, z.block), :] = residual[
+                v, pl.ds(a * z.block, z.block), :
+            ]
     copies[1].wait()
 
     def operators(r, _):
@@ -153,7 +144,7 @@
             d = [diag[i * z.v + j, pl.ds(r, z.cells, stride=z.rows), :] for j in span]
             for k in span:
                 for which in range(2):
-                    ops[r, which * vv + i * z.v + k] = -total(
+                    ops[r, which * vv + i * z.v + k] = total(
                         [d[j] * splats[which * vv + j * z.v + k] for j in span]
                     )
                 ops[r, 2 * vv + i * z.v + k] = d[k]
@@ -198,27 +189,17 @@
             outs[part][m] = maps[m, pl.ds(part * z.chunk, z.chunk), :]
 
 
-def prepare_kernel(z, *refs):
-    residual_h, prior_h, char_h, high_h, low_h, coupling_h, cutoffs_h, after = refs[:8]
-    source, spec, table_high, table_low, coupling, residual, prior, char, cutoffs, sems = refs[8:]
-    del after
+def prepare_kernel(z, prior, residual, coupling, *refs):
+    ins, refs = refs[:4], refs[4:]
+    source, spec, splats, table_high, table_low, char, cutoffs, sems = refs
+    held = [char, cutoffs, table_high, table_low]
+    copies = [
+        pltpu.make_async_copy(a, b, sems.at[k]) for k, (a, b) in enumerate(zip(ins, held))
+    ]
+    for copy in copies:
+        copy.start()
     span = range(z.v)
     vv = z.vv
-    pairs = [
-        (prior_h, prior),
-        (residual_h, residual),
-        (char_h, char),
-        (high_h, table_high),
-        (low_h, table_low),
-        (coupling_h, coupling),
-        (cutoffs_h, cutoffs),
-    ]
-    copies = [pltpu.make_async_copy(a, b, sems.at[k]) for k, (a, b) in enumerate(pairs)]
-    for copy in copies:
-        copy.start()
-
-    for k in (5, 6, 0, 1):
-        copies[k].wait()
     shape = (z.rows, LANES)
     factors = {
         (which, i, j): splat(coupling, which, i, j, shape)
@@ -226,6 +207,10 @@
         for i in span
         for j in span
     }
+    for which in range(2, 4):
+        for i in span:
+            for j in span:
+                splats[(which - 2) * vv + i * z.v + j] = factors[which, i, j]
 
     def scalar(which, i, j):
         return factors[which, i, j]
@@ -257,32 +242,31 @@
                     value = value - total([field[j] * scalar(which, i, j) for j in span])
                 source[i, pl.ds(a * z.block + h * z.rows, z.rows), :] = value
 
+    place = lax.broadcasted_iota(jnp.int32, (1, z.harmonics), 1)
+    harmonic = (place % z.per) * z.n + place // z.per
     k_of = lax.broadcasted_iota(jnp.int32, (z.harmonics, z.harmonics), 0)
-    place = lax.broadcasted_iota(jnp.int32, (z.harmonics, z.harmonics), 1)
-    wanted = (place % z.per) * z.n + place // z.per
-    select = jnp.where(k_of == wanted, 1.0, 0.0).astype(BF16)
-    copies[2].wait()
-    for c in range(2):
-        value = char[:, c, :]
-        high, rest = split(value)
-        rest = value - high.astype(F32)
-        middle, low = split(rest)
-        ordered = total(
-            [jnp.dot(part, select, preferred_element_type=F32) for part in (high, middle, low)]
-        )
-        row = lax.broadcasted_iota(jnp.int32, ordered.shape, 0)
-        place = lax.broadcasted_iota(jnp.int32, ordered.shape, 1)
-        harmonic = (place % z.per) * z.n + place // z.per
-        cutoff = jnp.where(row < vv, cutoffs[0], cutoffs[1])
-        weight = jnp.where(harmonic == 0, 1.0, 2.0) / z.points
-        spec[c] = ordered * jnp.where(harmonic < cutoff, weight, 0.0)
-    copies[3].wait()
-    copies[4].wait()
+    select = jnp.where(k_of == harmonic, 1.0, 0.0).astype(BF16)
+    for copy in copies[:2]:
+        copy.wait()
+    value = jnp.concatenate([char[:, c, :] for c in range(2)], axis=0)
+    high = value.astype(BF16)
+    middle, low = split(value - high.astype(F32))
+    ordered = total(
+        [jnp.dot(part, select, preferred_element_type=F32) for part in (high, middle, low)]
+    )
+    weight = jnp.where(harmonic == 0, 1.0, 2.0) / z.points
+    for q in range(2):
+        factor = jnp.where(harmonic < cutoffs[:, q : q + 1], weight, 0.0)
+        for c in range(2):
+            first = (2 * c + q) * vv
+            spec[c, pl.ds(q * vv, vv), :] = ordered[first : first + vv] * factor
+    for copy in copies[2:]:
+        copy.wait()
 
 
 def spectral_kernel(z, *refs):
     blocks = refs[: z.n]
-    table_high, table_low, spec, ops, source, coupling, driven, vectors, real, imag, total_source = (
+    table_high, table_low, spec, ops, source, splats, driven, vectors, real, imag, total_source = (
         refs[z.n :]
     )
     span = range(z.v)
@@ -290,7 +274,10 @@
     flat = 2 * z.v * z.rows
 
     def scalar(which, i, j):
-        return coupling[i, which : which + 1, j : j + 1]
+        return splats[(which - 2) * vv + i * z.v + j]
+
+    def column(halo, at):
+        return jnp.broadcast_to(halo[:, at : at + 1], (z.rows, LANES))
 
     def plane(ref):
         value = ref[pl.ds(0, z.planes), :].reshape(2 * z.v, z.tiles, z.rows, LANES)
@@ -363,8 +350,8 @@
     before = blocks[z.n - 1][pl.ds(z.planes, z.rows), :]
     after = blocks[1][pl.ds(z.planes, z.rows), :]
     for a in range(z.axial):
-        lows = [before[:, HALF + v * z.axial + a : HALF + v * z.axial + a + 1] for v in span]
-        highs = [after[:, v * z.axial + a : v * z.axial + a + 1] for v in span]
+        lows = [column(before, HALF + v * z.axial + a) for v in span]
+        highs = [column(after, v * z.axial + a) for v in span]
         for h in range(z.tiles):
             at = pl.ds(a * z.block + h * z.rows, z.rows)
             for i in span:
@@ -383,18 +370,15 @@
                         ]
                 total_source[i, at, :] = value
 
-    def drive(r, _):
+    stars = []
+    for r in range(z.rows):
         row = [total_source[j, pl.ds(r, z.cells, stride=z.rows), :] for j in span]
         new = matvec(lambda i, j: ops[r, 2 * vv + i * z.v + j], row)
         for i in span:
             driven[r, i] = new[i]
-        return 0
-
-    lax.fori_loop(0, z.rows, drive, 0)
-    stars = [[driven[0, i] for i in span]]
-    for r in range(1, z.rows):
-        moved = matvec(lambda i, j: ops[r, i * z.v + j], stars[-1])
-        stars.append([driven[r, i] + moved[i] for i in span])
+        if r:
+            new = plus(new, matvec(lambda i, j: ops[r, i * z.v + j], stars[-1]))
+        stars.append(new)
     back = stars[-1]
     for r in range(z.rows - 2, -1, -1):
         back = plus(stars[r], matvec(lambda i, j: ops[r, vv + i * z.v + j], back))
@@ -419,7 +403,7 @@
         fill(other, own)
 
 
-def merge_maps_kernel(z, level, last, device, own, other, out, slots):
+def merge_maps_kernel(z, level, device, own, other, out, slots):
     vv = z.vv
     every = list(range(3 * vv))
     place_pair((device[0] >> level) & 1, own, other, slots, every, every)
@@ -435,16 +419,42 @@
     for k in span:
         state = column(0, k)
         back = plus(column(vv, k), apply(2 * vv, apply(up + vv, state)))
-        if last:
-            for i in span:
-                out[i * z.v + k] = back[i]
-            continue
         state = apply(up, state)
         through = apply(2 * vv, column(up + 2 * vv, k))
         for i in span:
             out[i * z.v + k] = state[i]
             out[vv + i * z.v + k] = back[i]
             out[2 * vv + i * z.v + k] = through[i]
+
+
+def merge_last_kernel(z, level, device, *refs):
+    own_maps, other_maps = refs[: z.parts], refs[z.parts : 2 * z.parts]
+    own, other, out, state_out, slots, vectors = refs[2 * z.parts :]
+    vv = z.vv
+    span = range(z.v)
+    bit = (device[0] >> level) & 1
+    half = (device[0] >> (level + 1)) & 1
+    every = list(range(2 * z.v))
+    place_pair(bit, own, other, vectors, every, every)
+    lower, upper = range(3 * vv), range(2 * vv)
+    for part in range(z.parts):
+        at = pl.ds(part * z.chunk, z.chunk)
+        place_pair(bit, own_maps[part], other_maps[part], slots, lower, upper)
+
+        def apply(base, vector):
+            return matvec(lambda i, j: slots[base + i * z.v + j], vector)
+
+        fa, ha, fb, hb = [[vectors[k * z.v + i, at, :] for i in span] for k in range(4)]
+        state = plus(fb, apply(3 * vv, fa))
+        back = plus(ha, apply(2 * vv, plus(hb, apply(4 * vv, fa))))
+        for i in span:
+            state_out[i, at, :] = state[i]
+            out[i, at, :] = jnp.where(half == 0, state[i], back[i])
+        for k in span:
+            column = [slots[j * z.v + k] for j in span]
+            column = apply(2 * vv, apply(4 * vv, column))
+            for i in span:
+                out[z.v + i * z.v + k, at, :] = slots[vv + i * z.v + k] + column[i]
 
 
 def merge_vectors_kernel(z, level, device, *refs):
@@ -483,34 +493,36 @@
         return taken
 
     inner_maps = [(take(z.parts), take(z.parts)) for _ in range(levels - 1)]
-    outer = take(z.parts)
-    vector_pairs = [take(2) for _ in range(levels)]
-    ops, driven, out, slots, vectors, inside, stars = refs
+    vector_pairs = [take(2) for _ in range(levels - 1)]
+    own_state, told, ops, driven, out, slots, vectors, inside, stars = refs
 
     def load(base, at):
         return [inside[base + i, at, :] for i in span]
 
-    for level in range(levels - 1, -1, -1):
+    half = (device[0] >> (levels - 1)) & 1
+    word = [told[i] for i in span]
+    back = matvec(lambda i, j: told[z.v + i * z.v + j], [own_state[i] for i in span])
+    for i in span:
+        zero = jnp.zeros_like(word[i])
+        inside[i] = jnp.where(half == 0, zero, word[i])
+        inside[z.v + i] = jnp.where(half == 0, word[i] + back[i], zero)
+
+    for level in range(levels - 2, -1, -1):
         bit = (device[0] >> level) & 1
         own, other = vector_pairs[level]
         place_pair(bit, own, other, vectors, range(z.v), range(z.v, 2 * z.v))
         for part in range(z.parts):
             at = pl.ds(part * z.chunk, z.chunk)
             fa, hb = [[vectors[k * z.v + i, at, :] for i in span] for k in range(2)]
-            if level == levels - 1:
-                back = plus(hb, matvec(lambda i, j: outer[part][i * z.v + j], fa))
-                zero = [jnp.zeros_like(value) for value in fa]
-                xa, ya, xb, yb = zero, back, fa, zero
-            else:
-                own, other = inner_maps[level]
-                place_pair(bit, own[part], other[part], slots, range(vv), range(vv, 3 * vv))
-
-                def apply(base, vector):
-                    return matvec(lambda i, j: slots[base + i * z.v + j], vector)
-
-                xa, yb = load(0, at), load(z.v, at)
-                xb = plus(fa, apply(0, xa))
-                ya = plus(plus(hb, apply(vv, xb)), apply(2 * vv, yb))
+            own, other = inner_maps[level]
+            place_pair(bit, own[part], other[part], slots, range(vv), range(vv, 3 * vv))
+
+            def apply(base, vector):
+                return matvec(lambda i, j: slots[base + i * z.v + j], vector)
+
+            xa, yb = load(0, at), load(z.v, at)
+            xb = plus(fa, apply(0, xa))
+            ya = plus(plus(hb, apply(vv, xb)), apply(2 * vv, yb))
             for i in span:
                 inside[i, at, :] = jnp.where(bit == 0, xa[i], xb[i])
                 inside[z.v + i, at, :] = jnp.where(bit == 0, ya[i], yb[i])
@@ -539,9 +551,9 @@
     return high, low
 
 
-def exchange(value, span, level, both=True):
-    pairs = [(d ^ (1 << level), d) for d in range(span) if both or not (d >> level) & 1]
-    return lax.ppermute(value, "span", pairs)
+def exchange(value, span, level, mirrored=False):
+    flip = (2 << level) - 2 if mirrored else 1 << level
+    return lax.ppermute(value, "span", [(d ^ flip, d) for d in range(span)])
 
 
 def body(residual, inverse_diagonal, prior_increment, coupling, characteristic, cutoffs):
@@ -559,75 +571,60 @@
     field = (z.v, z.axial * z.block, LANES)
     scratch = pltpu.VMEM
 
-    payload = call(
-        functools.partial(payload_kernel, z),
-        [(z.planes + z.rows, LANES)],
-        (residual_t, prior_t),
-        [HBM] * 2,
-        [scratch(field, F32), pltpu.SemaphoreType.DMA((2 * z.v + 1,))],
-    )[0]
+    high, low = [jnp.asarray(table) for table in trig_tables(z)]
+    residual_t, prior_t, couple, payload, ops, *maps = call(
+        functools.partial(opening_kernel, z),
+        [field, field, couple.shape, (z.planes + z.rows, LANES), (z.rows, 3 * vv) + cell]
+        + [(3 * vv,) + part_cell] * z.parts,
+        (couple, diag_t, prior_t, residual_t),
+        [HBM] * 4,
+        [
+            scratch((3 * vv,) + cell, F32),
+            scratch((z.rows, vv) + cell, F32),
+            scratch(diag_t.shape, F32),
+            scratch((2 * vv,) + cell, F32),
+            pltpu.SemaphoreType.DMA((4,)),
+        ],
+        flops=10_000_000,
+    )
     blocks = [payload]
     for j in range(1, pitch):
         pairs = [((e + j) % pitch, e) for e in range(pitch)]
         blocks.append(lax.ppermute(payload, "pitch", pairs))
 
-    ops, *maps = call(
-        functools.partial(maps_kernel, z),
-        [(z.rows, 3 * vv) + cell] + [(3 * vv,) + part_cell] * z.parts,
-        (diag_t, couple, payload),
-        [HBM, HBM, ANY],
-        [
-            scratch((3 * vv,) + cell, F32),
-            scratch((z.rows, vv) + cell, F32),
-            scratch(diag_t.shape, F32),
-            scratch(couple.shape, F32),
-            scratch((2 * vv,) + cell, F32),
-            pltpu.SemaphoreType.DMA((2,)),
-        ],
-        flops=10_000_000,
-    )
     map_levels = []
-    for level in range(levels):
-        last = level == levels - 1
+    for level in range(levels - 1):
         others = []
         for value in maps:
-            others.append(exchange(value, span, level, not last))
+            others.append(exchange(value, span, level))
         map_levels.append((maps, others))
-        if last:
-            break
-        count = vv if level == levels - 2 else 3 * vv
-        maps = [
-            call(
-                functools.partial(merge_maps_kernel, z, level, level == levels - 2),
-                [(count,) + part_cell],
-                (device, mine, other),
-                [SMEM, VMEM, VMEM],
-                [scratch((6 * vv,) + part_cell, F32)],
-            )[0]
-            for mine, other in zip(maps, others)
-        ]
-
-    high, low = trig_tables(z)
-    source, spec, high, low, couple = call(
+        if level + 2 < levels:
+            maps = [
+                call(
+                    functools.partial(merge_maps_kernel, z, level),
+                    [(3 * vv,) + part_cell],
+                    (device, mine, other),
+                    [SMEM, VMEM, VMEM],
+                    [scratch((6 * vv,) + part_cell, F32)],
+                )[0]
+                for mine, other in zip(maps, others)
+            ]
+
+    source, spec, splats, high, low = call(
         functools.partial(prepare_kernel, z),
-        [field, (2, 2 * vv, z.harmonics), (high.shape, BF16), (low.shape, BF16), couple.shape],
-        (
-            residual_t,
-            prior_t,
-            char,
-            jnp.asarray(high),
-            jnp.asarray(low),
-            couple,
-            cutoffs,
-            payload,
-        ),
-        [HBM] * 7 + [ANY],
         [
-            scratch(field, F32),
-            scratch(field, F32),
+            field,
+            (2, 2 * vv, z.harmonics),
+            (2 * vv, z.rows, LANES),
+            (high.shape, BF16),
+            (low.shape, BF16),
+        ],
+        (prior_t, residual_t, couple, char, cutoffs.reshape(1, 2), high, low),
+        [VMEM] * 3 + [HBM] * 4,
+        [
             scratch(char.shape, F32),
-            pltpu.SMEM(cutoffs.shape, jnp.int32),
-            pltpu.SemaphoreType.DMA((7,)),
+            scratch((1, 2), jnp.int32),
+            pltpu.SemaphoreType.DMA((4,)),
         ],
         flops=5_000_000,
     )
@@ -636,7 +633,7 @@
     driven, vectors = call(
         functools.partial(spectral_kernel, z),
         [(z.rows, z.v) + cell, (2 * z.v,) + cell],
-        (*blocks, high, low, spec, ops, source, couple),
+        (*blocks, high, low, spec, ops, source, splats),
         [VMEM] * (z.n + 6),
         [
             scratch((rows, z.harmonics), F32),
@@ -647,25 +644,36 @@
     )
 
     vector_levels = []
-    for level in range(levels):
+    for level in range(levels - 1):
         other = exchange(vectors, span, level)
         vector_levels.append((vectors, other))
-        if level + 1 < levels:
-            mine, others = map_levels[level]
+        mine, others = map_levels[level]
+        ins = (device, *mine, *others, vectors, other)
+        specs = [SMEM] + [VMEM] * (2 * z.parts + 2)
+        if level + 2 < levels:
             vectors = call(
                 functools.partial(merge_vectors_kernel, z, level),
                 [(2 * z.v,) + cell],
-                (device, *mine, *others, vectors, other),
-                [SMEM] + [VMEM] * (2 * z.parts + 2),
+                ins,
+                specs,
                 [scratch((3 * vv,) + part_cell, F32), scratch((4 * z.v,) + cell, F32)],
             )[0]
+        else:
+            tell, state = call(
+                functools.partial(merge_last_kernel, z, level),
+                [(z.v + vv,) + cell, (z.v,) + cell],
+                ins,
+                specs,
+                [scratch((5 * vv,) + part_cell, F32), scratch((4 * z.v,) + cell, F32)],
+            )
+    told = exchange(tell, span, levels - 1, MIRRORED)
 
     arrays = []
-    for mine, others in map_levels[:-1]:
+    for mine, others in map_levels:
         arrays += [*mine, *others]
-    arrays += map_levels[-1][1]
     for pair in vector_levels:
         arrays += pair
+    arrays += [state, told]
     update = call(
         functools.partial(final_kernel, z, levels),
         [field],

time: 41 us -> 39.4 us (0.961)
  Pallas kernels: 12 us -> 7.12 us
  waiting for transfers between devices: 16.2 us -> 20.9 us
  starting transfers between devices: 12.5 us -> 11.1 us
    pallas_call x9 -> x7, Pallas kernels: 12 us -> 7.12 us  [kernel_call(): pl.pallas_call(kernel, out_shape=[jax.ShapeDtypeStruct(*s) if isinstance(...]
    ppermute x6 -> x5, waiting for transfers between devices: 14.6 us -> 17.8 us  [exchange(): return lax.ppermute(value, 'span', [(d ^ flip, d) for d in range(span)])]
    ppermute x3, waiting for transfers between devices: 1.66 us -> 3.18 us  [body(): blocks.append(lax.ppermute(payload, 'pitch', pairs))]
    ppermute x6 -> x5, starting transfers between devices: 10.8 us -> 9.41 us  [exchange(): return lax.ppermute(value, 'span', [(d ^ flip, d) for d in range(span)])]
  transfers between devices with their start and end apart: 9 -> 8, of which waited for: 6 -> 6; matrix products, arithmetic and copies ran while one was open for 0% -> 0% of each run, Pallas kernels for 17% -> 8%
where the time goes in v1:
time: 39.4 us; the launch traced here: 39.3 us
  waiting for transfers between devices  20.9 us (53%)
  starting transfers between devices  11.1 us (28%)
  Pallas kernels  7.12 us (18%)
    ppermute x5, waiting for transfers between devices, exchange(): return lax.ppermute(value, 'span', [(d ^ flip, d) for d in range(span)])  17.8 us
    ppermute x5, starting transfers between devices, exchange(): return lax.ppermute(value, 'span', [(d ^ flip, d) for d in range(span)])  9.41 us
    pallas_call x7, Pallas kernels, kernel_call(): pl.pallas_call(kernel, out_shape=[jax.ShapeDtypeStruct(*s) if isinstance(...  7.12 us
    ppermute x3, waiting for transfers between devices, body(): blocks.append(lax.ppermute(payload, 'pitch', pairs))  3.18 us
    ppermute x3, starting transfers between devices, body(): blocks.append(lax.ppermute(payload, 'pitch', pairs))  1.72 us
  transfers between devices with their start and end apart: 8, of which 6 were waited for; matrix products, arithmetic and copies ran while one was open for 0% of the time, Pallas kernels for 8%

profile of v1, /device:TPU:0, one launch (start us, length us, event | category | flops | bytes accessed | tf_op | source)
XLA Modules:
  0.0 39.3 jit_solution(15099487671807742830)
XLA Ops:
  0.0 2.8 %shard_map.82 = (f32[5,64,128]{2,1,0:T(8,128)S(1)}, f32[5,64,128]{2,1,0:T(8,128)S(1)}, f32[5,6,5]{2,1,0:T(8,128)S(1)}, f32[168,128]{1,0:T(8,128)S(1)}, f32[8,75,...) custom-call(f32[5,6,5]{2,1,0:T(8,128)} %bitcast.30, f32[25,64,128]{2,1,0:T(8,128)} %bitcast.26, f32[5,64,128]{2,1,0:T(8,128)} %bitcast.28, ...), custom_call_target="tpu_custom_call" | custom-call | flops 10000000 | bytes 1147480 | tf_op jit(solution)/shard_map/pallas_call | solution.py:35
  2.9 3.1 %collective-permute-start = (f32[75,8,128]{2,1,0:T(8,128)S(1)}, f32[75,8,128]{2,1,0:T(8,128)S(1)}, u32[]{:S(2)}, u32[]{:S(2)}) collective-permute-start(f32[75,8,128]{2,1,0:T(8,128)S(1)} %get-tuple-element.20.own.refs_0_), channel_id=1, source_target_pairs={{1,0},{0,1},{3,2},{2,3},{5,4},{4,5},{7,6},{6,7},{9,8},{8,9},{11,10... | collective-permute-start | bytes 921608 | tf_op jit(solution)/shard_map/ppermute | solution.py:556
  5.9 7.3 %collective-permute-done.other.refs_1_ = f32[75,8,128]{2,1,0:T(8,128)S(1)} collective-permute-done((f32[75,8,128]{2,1,0:T(8,128)S(1)}, f32[75,8,128]{2,1,0:T(8,128)S(1)}, u32[]{:S(2)}, u32[]{:S(2)}) %collective-permute-start) | collective-permute-done | bytes 307232 | tf_op jit(solution)/shard_map/ppermute | solution.py:556
  13.2 0.2 shard_map.83.refs_0_.refs_2_
  13.4 1.9 %collective-permute-start.1 = (f32[75,8,128]{2,1,0:T(8,128)S(1)}, f32[75,8,128]{2,1,0:T(8,128)S(1)}, u32[]{:S(2)}, u32[]{:S(2)}) collective-permute-start(f32[75,8,128]{2,1,0:T(8,128)S(1)} %shard_map.83.refs_0_.refs_2_), channel_id=1, source_target_pairs={{2,0},{3,1},{0,2},{1,3},{6,4},{7,5},{4,6},{5,7},{10,8},{11,9},{8,1... | collective-permute-start | bytes 921608 | tf_op jit(solution)/shard_map/ppermute | solution.py:556
  15.2 0.0 collective-permute-start.2
  15.2 1.5 %collective-permute-start.3 = (f32[168,128]{1,0:T(8,128)S(1)}, f32[168,128]{1,0:T(8,128)S(1)}, u32[]{:S(2)}, u32[]{:S(2)}) collective-permute-start(f32[168,128]{1,0:T(8,128)S(1)} %get-tuple-element.21.refs_0_), channel_id=1, source_target_pairs={{16,0},{24,8},{0,16},{8,24},{17,1},{25,9},{1,17},{9,25},{18,2},{26... | collective-permute-start | bytes 258056 | tf_op jit(solution)/shard_map/ppermute | solution.py:593
  16.7 0.2 collective-permute-start.4
  17.0 1.8 %shard_map.84 = (f32[5,64,128]{2,1,0:T(8,128)S(1)}, f32[2,50,512]{2,1,0:T(8,128)S(1)}, f32[50,8,128]{2,1,0:T(8,128)S(1)}, bf16[256,1024]{1,0:T(8,128)(2,1)S(1)}, bf16[256,1024]{1,0:T(8,128)(2,1)S(1)}) custom-call(f32[5,64,128]{2,1,0:T(8,128)S(1)} %get-tuple-element.22.prior, f32[5,64,128]{2,1,0:T(8,128)S(1)} %get-tuple-element.23.residual, ...), custom_call_target="tpu_custom_call" | custom-call | flops 5000000 | bytes 2630240 | tf_op jit(solution)/shard_map/pallas_call | solution.py:35
  18.8 0.0 collective-permute-done.2.refs_1_
  18.8 3.1 %collective-permute-done.3.refs_2_ = f32[168,128]{1,0:T(8,128)S(1)} collective-permute-done((f32[168,128]{1,0:T(8,128)S(1)}, f32[168,128]{1,0:T(8,128)S(1)}, u32[]{:S(2)}, u32[]{:S(2)}) %collective-permute-start.3) | collective-permute-done | bytes 86048 | tf_op jit(solution)/shard_map/ppermute | solution.py:593
  21.9 0.1 collective-permute-done.4.refs_3_
  21.9 1.2 %shard_map.85 = (f32[8,5,8,128]{3,2,1,0:T(8,128)S(1)}, f32[10,8,128]{2,1,0:T(8,128)S(1)}) custom-call(f32[168,128]{1,0:T(8,128)S(1)} %get-tuple-element.21.refs_0_, f32[168,128]{1,0:T(8,128)S(1)} %collective-permute-done.2.refs_1_, f32[168,128]{1,0:T(8,128)S(1)} %collective-permute-done.3.refs_2_, f32[168,128]{1,0:T(8,128)S(1)} %collective-permute-done.4.refs_3_, ...), custom_call_target="tpu_custom_call" | custom-call | flops 10000000 | bytes 5472256 | tf_op jit(solution)/shard_map/pallas_call | solution.py:35
  23.2 1.6 %collective-permute-start.5 = (f32[10,8,128]{2,1,0:T(8,128)S(1)}, f32[10,8,128]{2,1,0:T(8,128)S(1)}, u32[]{:S(2)}, u32[]{:S(2)}) collective-permute-start(f32[10,8,128]{2,1,0:T(8,128)S(1)} %get-tuple-element.31.refs_2_.refs_4_), channel_id=1, source_target_pairs={{1,0},{0,1},{3,2},{2,3},{5,4},{4,5},{7,6},{6,7},{9,8},{8,9},{11,10... | collective-permute-start | bytes 122888 | tf_op jit(solution)/shard_map/ppermute | solution.py:556
  24.7 2.5 %collective-permute-done.5.refs_3_.refs_5_ = f32[10,8,128]{2,1,0:T(8,128)S(1)} collective-permute-done((f32[10,8,128]{2,1,0:T(8,128)S(1)}, f32[10,8,128]{2,1,0:T(8,128)S(1)}, u32[]{:S(2)}, u32[]{:S(2)}) %collective-permute-start.5) | collective-permute-done | bytes 40992 | tf_op jit(solution)/shard_map/ppermute | solution.py:556
  27.2 0.1 shard_map.86.refs_2_.refs_6_
  27.3 0.4 collective-permute-start.6
  27.7 3.7 %collective-permute-done.6.refs_3_.refs_7_ = f32[10,8,128]{2,1,0:T(8,128)S(1)} collective-permute-done((f32[10,8,128]{2,1,0:T(8,128)S(1)}, f32[10,8,128]{2,1,0:T(8,128)S(1)}, u32[]{:S(2)}, u32[]{:S(2)}) %collective-permute-start.6) | collective-permute-done | bytes 40992 | tf_op jit(solution)/shard_map/ppermute | solution.py:556
  31.4 0.0 collective-permute-done.1.refs_1_.refs_3_
  31.4 0.1 shard_map.87
  31.5 2.5 %collective-permute-start.7 = (f32[30,8,128]{2,1,0:T(8,128)S(1)}, f32[30,8,128]{2,1,0:T(8,128)S(1)}, u32[]{:S(2)}, u32[]{:S(2)}) collective-permute-start(f32[30,8,128]{2,1,0:T(8,128)S(1)} %get-tuple-element.33), channel_id=1, source_target_pairs={{6,0},{7,1},{4,2},{5,3},{2,4},{3,5},{0,6},{1,7},{14,8},{15,9},{12,... | collective-permute-start | bytes 368648 | tf_op jit(solution)/shard_map/ppermute | solution.py:556
  34.0 4.3 %collective-permute-done.7.refs_9_ = f32[30,8,128]{2,1,0:T(8,128)S(1)} collective-permute-done((f32[30,8,128]{2,1,0:T(8,128)S(1)}, f32[30,8,128]{2,1,0:T(8,128)S(1)}, u32[]{:S(2)}, u32[]{:S(2)}) %collective-permute-start.7) | collective-permute-done | bytes 122912 | tf_op jit(solution)/shard_map/ppermute | solution.py:556
  38.3 0.9 %shard_map.88 = f32[5,64,128]{2,1,0:T(8,128)} custom-call(s32[1]{0:T(128)} %bitcast.device, f32[75,8,128]{2,1,0:T(8,128)S(1)} %get-tuple-element.20.own.refs_0_, f32[75,8,128]{2,1,0:T(8,128)S(1)} %collective-permute-done.other.refs_1_, f32[75,8,128]{2,1,0:T(8,128)S(1)} %shard_map.83.refs_0_.refs_2_, ...), custom_call_target="tpu_custom_call" | custom-call | flops 2000000 | bytes 4157444 | tf_op jit(solution)/shard_map/pallas_call | solution.py:35
Async XLA Ops:
  2.9 10.3 %collective-permute-start = (f32[75,8,128]{2,1,0:T(8,128)S(1)}, f32[75,8,128]{2,1,0:T(8,128)S(1)}, u32[]{:S(2)}, u32[]{:S(2)}) collective-permute-start(f32[75,8,128]{2,1,0:T(8,128)S(1)} %get-tuple-element.20.own.refs_0_), channel_id=1, source_target_pairs={{1,0},{0,1},{3,2},{2,3},{5,4},{4,5},{7,6},{6,7},{9,8},{8,9},{11,10... | collective-permute-start | bytes 921608 | tf_op jit(solution)/shard_map/ppermute | solution.py:556
  13.4 18.0 %collective-permute-start.1 = (f32[75,8,128]{2,1,0:T(8,128)S(1)}, f32[75,8,128]{2,1,0:T(8,128)S(1)}, u32[]{:S(2)}, u32[]{:S(2)}) collective-permute-start(f32[75,8,128]{2,1,0:T(8,128)S(1)} %shard_map.83.refs_0_.refs_2_), channel_id=1, source_target_pairs={{2,0},{3,1},{0,2},{1,3},{6,4},{7,5},{4,6},{5,7},{10,8},{11,9},{8,1... | collective-permute-start | bytes 921608 | tf_op jit(solution)/shard_map/ppermute | solution.py:556
  15.2 3.5 %collective-permute-start.2 = (f32[168,128]{1,0:T(8,128)S(1)}, f32[168,128]{1,0:T(8,128)S(1)}, u32[]{:S(2)}, u32[]{:S(2)}) collective-permute-start(f32[168,128]{1,0:T(8,128)S(1)} %get-tuple-element.21.refs_0_), channel_id=1, source_target_pairs={{8,0},{16,8},{24,16},{0,24},{9,1},{17,9},{25,17},{1,25},{10,2},{18... | collective-permute-start | bytes 258056 | tf_op jit(solution)/shard_map/ppermute | solution.py:593
  15.2 6.6 %collective-permute-start.3 = (f32[168,128]{1,0:T(8,128)S(1)}, f32[168,128]{1,0:T(8,128)S(1)}, u32[]{:S(2)}, u32[]{:S(2)}) collective-permute-start(f32[168,128]{1,0:T(8,128)S(1)} %get-tuple-element.21.refs_0_), channel_id=1, source_target_pairs={{16,0},{24,8},{0,16},{8,24},{17,1},{25,9},{1,17},{9,25},{18,2},{26... | collective-permute-start | bytes 258056 | tf_op jit(solution)/shard_map/ppermute | solution.py:593
  16.7 5.2 %collective-permute-start.4 = (f32[168,128]{1,0:T(8,128)S(1)}, f32[168,128]{1,0:T(8,128)S(1)}, u32[]{:S(2)}, u32[]{:S(2)}) collective-permute-start(f32[168,128]{1,0:T(8,128)S(1)} %get-tuple-element.21.refs_0_), channel_id=1, source_target_pairs={{24,0},{0,8},{8,16},{16,24},{25,1},{1,9},{9,17},{17,25},{26,2},{2,... | collective-permute-start | bytes 258056 | tf_op jit(solution)/shard_map/ppermute | solution.py:593
  23.2 4.1 %collective-permute-start.5 = (f32[10,8,128]{2,1,0:T(8,128)S(1)}, f32[10,8,128]{2,1,0:T(8,128)S(1)}, u32[]{:S(2)}, u32[]{:S(2)}) collective-permute-start(f32[10,8,128]{2,1,0:T(8,128)S(1)} %get-tuple-element.31.refs_2_.refs_4_), channel_id=1, source_target_pairs={{1,0},{0,1},{3,2},{2,3},{5,4},{4,5},{7,6},{6,7},{9,8},{8,9},{11,10... | collective-permute-start | bytes 122888 | tf_op jit(solution)/shard_map/ppermute | solution.py:556
  27.3 4.1 %collective-permute-start.6 = (f32[10,8,128]{2,1,0:T(8,128)S(1)}, f32[10,8,128]{2,1,0:T(8,128)S(1)}, u32[]{:S(2)}, u32[]{:S(2)}) collective-permute-start(f32[10,8,128]{2,1,0:T(8,128)S(1)} %shard_map.86.refs_2_.refs_6_), channel_id=1, source_target_pairs={{2,0},{3,1},{0,2},{1,3},{6,4},{7,5},{4,6},{5,7},{10,8},{11,9},{8,1... | collective-permute-start | bytes 122888 | tf_op jit(solution)/shard_map/ppermute | solution.py:556
  31.5 6.8 %collective-permute-start.7 = (f32[30,8,128]{2,1,0:T(8,128)S(1)}, f32[30,8,128]{2,1,0:T(8,128)S(1)}, u32[]{:S(2)}, u32[]{:S(2)}) collective-permute-start(f32[30,8,128]{2,1,0:T(8,128)S(1)} %get-tuple-element.33), channel_id=1, source_target_pairs={{6,0},{7,1},{4,2},{5,3},{2,4},{3,5},{0,6},{1,7},{14,8},{15,9},{12,... | collective-permute-start | bytes 368648 | tf_op jit(solution)/shard_map/ppermute | solution.py:556

commit v2 on v1

--- a/solution.py
+++ b/solution.py
@@ -16,7 +16,7 @@
 SMEM = pl.BlockSpec(memory_space=pltpu.SMEM)
 HBM = pl.BlockSpec(memory_space=pltpu.HBM)
 ANY = pl.BlockSpec(memory_space=pl.ANY)
-PARTS = 1
+PARTS = 2
 MIRRORED = True
 F32 = jnp.float32
 BF16 = jnp.bfloat16
@@ -102,17 +102,19 @@
 
 
 def opening_kernel(z, *refs):
-    ins, refs = refs[:4], refs[4:]
+    ins, refs = refs[:4], refs[5:]
     residual, prior, coupling, payload, ops = refs[:5]
     outs, (maps, powers, diag, splats, sems) = refs[5 : 5 + z.parts], refs[5 + z.parts :]
-    held = [coupling, diag, prior, residual]
-    copies = [
-        pltpu.make_async_copy(a, b, sems.at[k]) for k, (a, b) in enumerate(zip(ins, held))
-    ]
-    for copy in copies:
-        copy.start()
     span = range(z.v)
     vv = z.vv
+    coupling_h, diag_h, prior_h, residual_h = ins
+    pairs = [(coupling_h, coupling), (prior_h, prior), (residual_h, residual)]
+    for i in span:
+        at = pl.ds(i * z.v, z.v)
+        pairs.append((diag_h.at[at], diag.at[at]))
+    copies = [pltpu.make_async_copy(a, b, sems.at[k]) for k, (a, b) in enumerate(pairs)]
+    for k in (0, 1, 2, 3, 4, 5, 6, 7):
+        copies[k].start()
 
     copies[0].wait()
     for which in range(2):
@@ -121,7 +123,7 @@
                 splats[which * vv + i * z.v + j] = -splat(
                     coupling, which, i, j, (z.cells, LANES)
                 )
-    copies[2].wait()
+    copies[1].wait()
     lane = lax.broadcasted_iota(jnp.int32, (z.rows, LANES), 1)
     halo = jnp.zeros((z.rows, LANES), F32)
     for v in span:
@@ -131,16 +133,17 @@
             halo = jnp.where(lane == v * z.axial + a, first, halo)
             halo = jnp.where(lane == HALF + v * z.axial + a, last, halo)
     payload[pl.ds(z.planes, z.rows), :] = halo
-    copies[3].wait()
+    copies[2].wait()
     for q, a in enumerate((0, z.axial - 1)):
         for v in span:
             payload[pl.ds((q * z.v + v) * z.block, z.block), :] = residual[
                 v, pl.ds(a * z.block, z.block), :
             ]
-    copies[1].wait()
-
-    def operators(r, _):
-        for i in span:
+
+    for i in span:
+        copies[3 + i].wait()
+
+        def operators(r, _, i=i):
             d = [diag[i * z.v + j, pl.ds(r, z.cells, stride=z.rows), :] for j in span]
             for k in span:
                 for which in range(2):
@@ -148,9 +151,9 @@
                         [d[j] * splats[which * vv + j * z.v + k] for j in span]
                     )
                 ops[r, 2 * vv + i * z.v + k] = d[k]
-        return 0
-
-    lax.fori_loop(0, z.rows, operators, 0)
+            return 0
+
+        lax.fori_loop(0, z.rows, operators, 0, unroll=True)
 
     for m in range(vv):
         powers[0, m] = ops[0, m]
@@ -163,7 +166,7 @@
                 powers[r, i * z.v + k] = new[i]
         return 0
 
-    lax.fori_loop(1, z.rows, forward, 0)
+    lax.fori_loop(1, z.rows, forward, 0, unroll=True)
     top = z.rows - 1
     for m in range(vv):
         maps[m] = powers[top, m]
@@ -183,7 +186,7 @@
                     maps[base + i * z.v + k] = value
         return 0
 
-    lax.fori_loop(1, z.rows, backward, 0)
+    lax.fori_loop(1, z.rows, backward, 0, unroll=True)
     for part in range(z.parts):
         for m in range(3 * vv):
             outs[part][m] = maps[m, pl.ds(part * z.chunk, z.chunk), :]
@@ -427,6 +430,21 @@
             out[2 * vv + i * z.v + k] = through[i]
 
 
+def merge_response_kernel(z, level, device, own, other, out, slots):
+    vv = z.vv
+    place_pair((device[0] >> level) & 1, own, other, slots, range(3 * vv), range(2 * vv))
+    span = range(z.v)
+
+    def apply(base, vector):
+        return matvec(lambda i, j: slots[base + i * z.v + j], vector)
+
+    for k in span:
+        column = [slots[j * z.v + k] for j in span]
+        column = apply(2 * vv, apply(4 * vv, column))
+        for i in span:
+            out[i * z.v + k] = slots[vv + i * z.v + k] + column[i]
+
+
 def merge_last_kernel(z, level, device, *refs):
     own_maps, other_maps = refs[: z.parts], refs[z.parts : 2 * z.parts]
     own, other, out, state_out, slots, vectors = refs[2 * z.parts :]
@@ -449,12 +467,14 @@
         back = plus(ha, apply(2 * vv, plus(hb, apply(4 * vv, fa))))
         for i in span:
             state_out[i, at, :] = state[i]
-            out[i, at, :] = jnp.where(half == 0, state[i], back[i])
+            out[part * z.v + i] = jnp.where(half == 0, state[i], back[i])
+        if part + 1 < z.parts:
+            continue
         for k in span:
             column = [slots[j * z.v + k] for j in span]
             column = apply(2 * vv, apply(4 * vv, column))
             for i in span:
-                out[z.v + i * z.v + k, at, :] = slots[vv + i * z.v + k] + column[i]
+                out[z.parts * z.v + i * z.v + k] = slots[vv + i * z.v + k] + column[i]
 
 
 def merge_vectors_kernel(z, level, device, *refs):
@@ -494,18 +514,23 @@
 
     inner_maps = [(take(z.parts), take(z.parts)) for _ in range(levels - 1)]
     vector_pairs = [take(2) for _ in range(levels - 1)]
+    responses = take(z.parts - 1)
     own_state, told, ops, driven, out, slots, vectors, inside, stars = refs
 
     def load(base, at):
         return [inside[base + i, at, :] for i in span]
 
     half = (device[0] >> (levels - 1)) & 1
-    word = [told[i] for i in span]
-    back = matvec(lambda i, j: told[z.v + i * z.v + j], [own_state[i] for i in span])
-    for i in span:
-        zero = jnp.zeros_like(word[i])
-        inside[i] = jnp.where(half == 0, zero, word[i])
-        inside[z.v + i] = jnp.where(half == 0, word[i] + back[i], zero)
+    for part in range(z.parts):
+        at = pl.ds(part * z.chunk, z.chunk)
+        word = [told[part * z.v + i] for i in span]
+        g, base = (responses[part], 0) if part + 1 < z.parts else (told, z.parts * z.v)
+        state = [own_state[i, at, :] for i in span]
+        back = matvec(lambda i, j: g[base + i * z.v + j], state)
+        for i in span:
+            zero = jnp.zeros_like(word[i])
+            inside[i, at, :] = jnp.where(half == 0, zero, word[i])
+            inside[z.v + i, at, :] = jnp.where(half == 0, word[i] + back[i], zero)
 
     for level in range(levels - 2, -1, -1):
         bit = (device[0] >> level) & 1
@@ -576,14 +601,14 @@
         functools.partial(opening_kernel, z),
         [field, field, couple.shape, (z.planes + z.rows, LANES), (z.rows, 3 * vv) + cell]
         + [(3 * vv,) + part_cell] * z.parts,
-        (couple, diag_t, prior_t, residual_t),
-        [HBM] * 4,
+        (couple, diag_t, prior_t, residual_t, device),
+        [HBM] * 4 + [SMEM],
         [
             scratch((3 * vv,) + cell, F32),
             scratch((z.rows, vv) + cell, F32),
             scratch(diag_t.shape, F32),
             scratch((2 * vv,) + cell, F32),
-            pltpu.SemaphoreType.DMA((4,)),
+            pltpu.SemaphoreType.DMA((8,)),
         ],
         flops=10_000_000,
     )
@@ -661,11 +686,22 @@
         else:
             tell, state = call(
                 functools.partial(merge_last_kernel, z, level),
-                [(z.v + vv,) + cell, (z.v,) + cell],
+                [(z.parts * z.v + vv,) + part_cell, (z.v,) + cell],
                 ins,
                 specs,
                 [scratch((5 * vv,) + part_cell, F32), scratch((4 * z.v,) + cell, F32)],
             )
+    responses = []
+    for part in range(z.parts - 1):
+        given = [side[part] for side in map_levels[-1]]
+        response = call(
+            functools.partial(merge_response_kernel, z, levels - 2),
+            [(vv,) + part_cell],
+            (device, *given),
+            [SMEM, VMEM, VMEM],
+            [scratch((5 * vv,) + part_cell, F32)],
+        )[0]
+        responses.append(exchange(response, span, levels - 1, MIRRORED))
     told = exchange(tell, span, levels - 1, MIRRORED)
 
     arrays = []
@@ -673,7 +709,7 @@
         arrays += [*mine, *others]
     for pair in vector_levels:
         arrays += pair
-    arrays += [state, told]
+    arrays += [*responses, state, told]
     update = call(
         functools.partial(final_kernel, z, levels),
         [field],

time: 39.4 us -> 36 us (0.914)
  waiting for transfers between devices: 20.9 us -> 13.6 us
  starting transfers between devices: 11.1 us -> 15.1 us
    ppermute x5 -> x8, waiting for transfers between devices: 17.8 us -> 13.6 us  [exchange(): return lax.ppermute(value, 'span', [(d ^ flip, d) for d in range(span)])]
    ppermute x5 -> x8, starting transfers between devices: 9.41 us -> 13 us  [exchange(): return lax.ppermute(value, 'span', [(d ^ flip, d) for d in range(span)])]
    ppermute x3, waiting for transfers between devices: 3.18 us -> 0.01 us  [body(): blocks.append(lax.ppermute(payload, 'pitch', pairs))]
    ppermute x3, starting transfers between devices: 1.72 us -> 2.15 us  [body(): blocks.append(lax.ppermute(payload, 'pitch', pairs))]
    pallas_call x7 -> x9, Pallas kernels: 7.12 us -> 7.03 us  [kernel_call(): pl.pallas_call(kernel, out_shape=[jax.ShapeDtypeStruct(*s) if isinstance(...]
  transfers between devices with their start and end apart: 8 -> 11, of which waited for: 6 -> 5; matrix products, arithmetic and copies ran while one was open for 0% -> 0% of each run, Pallas kernels for 8% -> 10%
where the time goes in v2:
time: 36 us; the launch traced here: 35.8 us
  starting transfers between devices  15.1 us (42%)
  waiting for transfers between devices  13.6 us (38%)
  Pallas kernels  7.03 us (20%)
    ppermute x8, waiting for transfers between devices, exchange(): return lax.ppermute(value, 'span', [(d ^ flip, d) for d in range(span)])  13.6 us
    ppermute x8, starting transfers between devices, exchange(): return lax.ppermute(value, 'span', [(d ^ flip, d) for d in range(span)])  13 us
    pallas_call x9, Pallas kernels, kernel_call(): pl.pallas_call(kernel, out_shape=[jax.ShapeDtypeStruct(*s) if isinstance(...  7.03 us
    ppermute x3, starting transfers between devices, body(): blocks.append(lax.ppermute(payload, 'pitch', pairs))  2.15 us
  transfers between devices with their start and end apart: 11, of which 5 were waited for; matrix products, arithmetic and copies ran while one was open for 0% of the time, Pallas kernels for 10%

profile of v2, /device:TPU:0, one launch (start us, length us, event | category | flops | bytes accessed | tf_op | source)
XLA Modules:
  0.0 35.8 jit_solution(16394617290616307469)
XLA Ops:
  0.0 2.4 %shard_map.82 = (f32[5,64,128]{2,1,0:T(8,128)S(1)}, f32[5,64,128]{2,1,0:T(8,128)S(1)}, f32[5,6,5]{2,1,0:T(8,128)S(1)}, f32[168,128]{1,0:T(8,128)S(1)}, f32[8,75,...) custom-call(f32[5,6,5]{2,1,0:T(8,128)} %bitcast.30, f32[25,64,128]{2,1,0:T(8,128)} %bitcast.26, ...), custom_call_target="tpu_custom_call" | custom-call | flops 10000000 | bytes 1147484 | tf_op jit(solution)/shard_map/pallas_call | solution.py:35
  2.4 3.1 %collective-permute-start = (f32[75,4,128]{2,1,0:T(4,128)S(1)}, f32[75,4,128]{2,1,0:T(4,128)S(1)}, u32[]{:S(2)}, u32[]{:S(2)}) collective-permute-start(f32[75,4,128]{2,1,0:T(4,128)S(1)} %get-tuple-element.21.own.refs_0_), channel_id=1, source_target_pairs={{1,0},{0,1},{3,2},{2,3},{5,4},{4,5},{7,6},{6,7},{9,8},{8,9},{11,10... | collective-permute-start | bytes 460808 | tf_op jit(solution)/shard_map/ppermute | solution.py:581
  5.5 0.1 collective-permute-start.1
  5.6 0.8 %collective-permute-start.4 = (f32[168,128]{1,0:T(8,128)S(1)}, f32[168,128]{1,0:T(8,128)S(1)}, u32[]{:S(2)}, u32[]{:S(2)}) collective-permute-start(f32[168,128]{1,0:T(8,128)S(1)} %get-tuple-element.23.refs_0_), channel_id=1, source_target_pairs={{8,0},{16,8},{24,16},{0,24},{9,1},{17,9},{25,17},{1,25},{10,2},{18... | collective-permute-start | bytes 258056 | tf_op jit(solution)/shard_map/ppermute | solution.py:618
  6.4 1.1 %collective-permute-start.5 = (f32[168,128]{1,0:T(8,128)S(1)}, f32[168,128]{1,0:T(8,128)S(1)}, u32[]{:S(2)}, u32[]{:S(2)}) collective-permute-start(f32[168,128]{1,0:T(8,128)S(1)} %get-tuple-element.23.refs_0_), channel_id=1, source_target_pairs={{16,0},{24,8},{0,16},{8,24},{17,1},{25,9},{1,17},{9,25},{18,2},{26... | collective-permute-start | bytes 258056 | tf_op jit(solution)/shard_map/ppermute | solution.py:618
  7.5 0.2 collective-permute-start.6
  7.7 2.6 %collective-permute-done.other.refs_2_ = f32[75,4,128]{2,1,0:T(4,128)S(1)} collective-permute-done((f32[75,4,128]{2,1,0:T(4,128)S(1)}, f32[75,4,128]{2,1,0:T(4,128)S(1)}, u32[]{:S(2)}, u32[]{:S(2)}) %collective-permute-start) | collective-permute-done | bytes 153632 | tf_op jit(solution)/shard_map/ppermute | solution.py:581
  10.3 0.2 shard_map.83.own.refs_0_.refs_4_
  10.5 2.1 %collective-permute-start.2 = (f32[75,4,128]{2,1,0:T(4,128)S(1)}, f32[75,4,128]{2,1,0:T(4,128)S(1)}, u32[]{:S(2)}, u32[]{:S(2)}) collective-permute-start(f32[75,4,128]{2,1,0:T(4,128)S(1)} %shard_map.83.own.refs_0_.refs_4_), channel_id=1, source_target_pairs={{2,0},{3,1},{0,2},{1,3},{6,4},{7,5},{4,6},{5,7},{10,8},{11,9},{8,1... | collective-permute-start | bytes 460808 | tf_op jit(solution)/shard_map/ppermute | solution.py:581
  12.6 0.1 collective-permute-done.1.other.refs_3_
  12.8 0.2 shard_map.84.refs_1_.refs_5_
  12.9 1.9 %collective-permute-start.3 = (f32[75,4,128]{2,1,0:T(4,128)S(1)}, f32[75,4,128]{2,1,0:T(4,128)S(1)}, u32[]{:S(2)}, u32[]{:S(2)}) collective-permute-start(f32[75,4,128]{2,1,0:T(4,128)S(1)} %shard_map.84.refs_1_.refs_5_), channel_id=1, source_target_pairs={{2,0},{3,1},{0,2},{1,3},{6,4},{7,5},{4,6},{5,7},{10,8},{11,9},{8,1... | collective-permute-start | bytes 460808 | tf_op jit(solution)/shard_map/ppermute | solution.py:581
  14.8 1.8 %shard_map.85 = (f32[5,64,128]{2,1,0:T(8,128)S(1)}, f32[2,50,512]{2,1,0:T(8,128)S(1)}, f32[50,8,128]{2,1,0:T(8,128)S(1)}, bf16[256,1024]{1,0:T(8,128)(2,1)S(1)}, bf16[256,1024]{1,0:T(8,128)(2,1)S(1)}) custom-call(f32[5,64,128]{2,1,0:T(8,128)S(1)} %get-tuple-element.24.prior, f32[5,64,128]{2,1,0:T(8,128)S(1)} %get-tuple-element.25.residual, ...), custom_call_target="tpu_custom_call" | custom-call | flops 5000000 | bytes 2630240 | tf_op jit(solution)/shard_map/pallas_call | solution.py:35
  16.6 0.0 collective-permute-done.4.refs_1_
  16.6 0.0 collective-permute-done.5.refs_2_
  16.6 0.0 collective-permute-done.6.refs_3_
  16.6 1.2 %shard_map.86 = (f32[8,5,8,128]{3,2,1,0:T(8,128)S(1)}, f32[10,8,128]{2,1,0:T(8,128)S(1)}) custom-call(f32[168,128]{1,0:T(8,128)S(1)} %get-tuple-element.23.refs_0_, f32[168,128]{1,0:T(8,128)S(1)} %collective-permute-done.4.refs_1_, f32[168,128]{1,0:T(8,128)S(1)} %collective-permute-done.5.refs_2_, f32[168,128]{1,0:T(8,128)S(1)} %collective-permute-done.6.refs_3_, ...), custom_call_target="tpu_custom_call" | custom-call | flops 10000000 | bytes 5472256 | tf_op jit(solution)/shard_map/pallas_call | solution.py:35
  17.8 1.6 %collective-permute-start.7 = (f32[10,8,128]{2,1,0:T(8,128)S(1)}, f32[10,8,128]{2,1,0:T(8,128)S(1)}, u32[]{:S(2)}, u32[]{:S(2)}) collective-permute-start(f32[10,8,128]{2,1,0:T(8,128)S(1)} %get-tuple-element.33.refs_4_.refs_8_), channel_id=1, source_target_pairs={{1,0},{0,1},{3,2},{2,3},{5,4},{4,5},{7,6},{6,7},{9,8},{8,9},{11,10... | collective-permute-start | bytes 122888 | tf_op jit(solution)/shard_map/ppermute | solution.py:581
  19.4 2.5 %collective-permute-done.7.refs_5_.refs_9_ = f32[10,8,128]{2,1,0:T(8,128)S(1)} collective-permute-done((f32[10,8,128]{2,1,0:T(8,128)S(1)}, f32[10,8,128]{2,1,0:T(8,128)S(1)}, u32[]{:S(2)}, u32[]{:S(2)}) %collective-permute-start.7) | collective-permute-done | bytes 40992 | tf_op jit(solution)/shard_map/ppermute | solution.py:581
  21.9 0.1 shard_map.87.refs_4_.refs_10_
  22.0 0.3 collective-permute-start.8
  22.3 3.8 %collective-permute-done.8.refs_5_.refs_11_ = f32[10,8,128]{2,1,0:T(8,128)S(1)} collective-permute-done((f32[10,8,128]{2,1,0:T(8,128)S(1)}, f32[10,8,128]{2,1,0:T(8,128)S(1)}, u32[]{:S(2)}, u32[]{:S(2)}) %collective-permute-start.8) | collective-permute-done | bytes 40992 | tf_op jit(solution)/shard_map/ppermute | solution.py:581
  26.0 0.0 collective-permute-done.2.other.refs_2_.refs_6_
  26.1 0.0 collective-permute-done.3.refs_3_.refs_7_
  26.1 0.2 shard_map.89
  26.2 2.5 %collective-permute-start.10 = (f32[35,4,128]{2,1,0:T(4,128)S(1)}, f32[35,4,128]{2,1,0:T(4,128)S(1)}, u32[]{:S(2)}, u32[]{:S(2)}) collective-permute-start(f32[35,4,128]{2,1,0:T(4,128)S(1)} %get-tuple-element.35), channel_id=1, source_target_pairs={{6,0},{7,1},{4,2},{5,3},{2,4},{3,5},{0,6},{1,7},{14,8},{15,9},{12,... | collective-permute-start | bytes 215048 | tf_op jit(solution)/shard_map/ppermute | solution.py:581
  28.8 0.1 shard_map.88
  28.9 1.4 %collective-permute-start.9 = (f32[25,4,128]{2,1,0:T(4,128)S(1)}, f32[25,4,128]{2,1,0:T(4,128)S(1)}, u32[]{:S(2)}, u32[]{:S(2)}) collective-permute-start(f32[25,4,128]{2,1,0:T(4,128)S(1)} %shard_map.88), channel_id=1, source_target_pairs={{6,0},{7,1},{4,2},{5,3},{2,4},{3,5},{0,6},{1,7},{14,8},{15,9},{12,... | collective-permute-start | bytes 153608 | tf_op jit(solution)/shard_map/ppermute | solution.py:581
  30.3 4.6 %collective-permute-done.9.refs_12_ = f32[25,4,128]{2,1,0:T(4,128)S(1)} collective-permute-done((f32[25,4,128]{2,1,0:T(4,128)S(1)}, f32[25,4,128]{2,1,0:T(4,128)S(1)}, u32[]{:S(2)}, u32[]{:S(2)}) %collective-permute-start.9) | collective-permute-done | bytes 51232 | tf_op jit(solution)/shard_map/ppermute | solution.py:581
  34.8 0.0 collective-permute-done.10.refs_14_
  34.8 1.0 %shard_map.90 = f32[5,64,128]{2,1,0:T(8,128)} custom-call(s32[1]{0:T(128)} %bitcast.refs_4_.device, f32[75,4,128]{2,1,0:T(4,128)S(1)} %get-tuple-element.21.own.refs_0_, f32[75,4,128]{2,1,0:T(4,128)S(1)} %get-tuple-element.22.own.refs_1_, f32[75,4,128]{2,1,0:T(4,128)S(1)} %collective-permute-done.other.refs_2_, ...), custom_call_target="tpu_custom_call" | custom-call | flops 2000000 | bytes 4157444 | tf_op jit(solution)/shard_map/pallas_call | solution.py:35
Async XLA Ops:
  2.4 7.9 %collective-permute-start = (f32[75,4,128]{2,1,0:T(4,128)S(1)}, f32[75,4,128]{2,1,0:T(4,128)S(1)}, u32[]{:S(2)}, u32[]{:S(2)}) collective-permute-start(f32[75,4,128]{2,1,0:T(4,128)S(1)} %get-tuple-element.21.own.refs_0_), channel_id=1, source_target_pairs={{1,0},{0,1},{3,2},{2,3},{5,4},{4,5},{7,6},{6,7},{9,8},{8,9},{11,10... | collective-permute-start | bytes 460808 | tf_op jit(solution)/shard_map/ppermute | solution.py:581
  5.5 7.3 %collective-permute-start.1 = (f32[75,4,128]{2,1,0:T(4,128)S(1)}, f32[75,4,128]{2,1,0:T(4,128)S(1)}, u32[]{:S(2)}, u32[]{:S(2)}) collective-permute-start(f32[75,4,128]{2,1,0:T(4,128)S(1)} %get-tuple-element.22.own.refs_1_), channel_id=1, source_target_pairs={{1,0},{0,1},{3,2},{2,3},{5,4},{4,5},{7,6},{6,7},{9,8},{8,9},{11,10... | collective-permute-start | bytes 460808 | tf_op jit(solution)/shard_map/ppermute | solution.py:581
  5.6 11.0 %collective-permute-start.4 = (f32[168,128]{1,0:T(8,128)S(1)}, f32[168,128]{1,0:T(8,128)S(1)}, u32[]{:S(2)}, u32[]{:S(2)}) collective-permute-start(f32[168,128]{1,0:T(8,128)S(1)} %get-tuple-element.23.refs_0_), channel_id=1, source_target_pairs={{8,0},{16,8},{24,16},{0,24},{9,1},{17,9},{25,17},{1,25},{10,2},{18... | collective-permute-start | bytes 258056 | tf_op jit(solution)/shard_map/ppermute | solution.py:618
  6.4 10.2 %collective-permute-start.5 = (f32[168,128]{1,0:T(8,128)S(1)}, f32[168,128]{1,0:T(8,128)S(1)}, u32[]{:S(2)}, u32[]{:S(2)}) collective-permute-start(f32[168,128]{1,0:T(8,128)S(1)} %get-tuple-element.23.refs_0_), channel_id=1, source_target_pairs={{16,0},{24,8},{0,16},{8,24},{17,1},{25,9},{1,17},{9,25},{18,2},{26... | collective-permute-start | bytes 258056 | tf_op jit(solution)/shard_map/ppermute | solution.py:618
  7.5 9.1 %collective-permute-start.6 = (f32[168,128]{1,0:T(8,128)S(1)}, f32[168,128]{1,0:T(8,128)S(1)}, u32[]{:S(2)}, u32[]{:S(2)}) collective-permute-start(f32[168,128]{1,0:T(8,128)S(1)} %get-tuple-element.23.refs_0_), channel_id=1, source_target_pairs={{24,0},{0,8},{8,16},{16,24},{25,1},{1,9},{9,17},{17,25},{26,2},{2,... | collective-permute-start | bytes 258056 | tf_op jit(solution)/shard_map/ppermute | solution.py:618
  10.5 15.6 %collective-permute-start.2 = (f32[75,4,128]{2,1,0:T(4,128)S(1)}, f32[75,4,128]{2,1,0:T(4,128)S(1)}, u32[]{:S(2)}, u32[]{:S(2)}) collective-permute-start(f32[75,4,128]{2,1,0:T(4,128)S(1)} %shard_map.83.own.refs_0_.refs_4_), channel_id=1, source_target_pairs={{2,0},{3,1},{0,2},{1,3},{6,4},{7,5},{4,6},{5,7},{10,8},{11,9},{8,1... | collective-permute-start | bytes 460808 | tf_op jit(solution)/shard_map/ppermute | solution.py:581
  12.9 13.1 %collective-permute-start.3 = (f32[75,4,128]{2,1,0:T(4,128)S(1)}, f32[75,4,128]{2,1,0:T(4,128)S(1)}, u32[]{:S(2)}, u32[]{:S(2)}) collective-permute-start(f32[75,4,128]{2,1,0:T(4,128)S(1)} %shard_map.84.refs_1_.refs_5_), channel_id=1, source_target_pairs={{2,0},{3,1},{0,2},{1,3},{6,4},{7,5},{4,6},{5,7},{10,8},{11,9},{8,1... | collective-permute-start | bytes 460808 | tf_op jit(solution)/shard_map/ppermute | solution.py:581
  17.8 4.1 %collective-permute-start.7 = (f32[10,8,128]{2,1,0:T(8,128)S(1)}, f32[10,8,128]{2,1,0:T(8,128)S(1)}, u32[]{:S(2)}, u32[]{:S(2)}) collective-permute-start(f32[10,8,128]{2,1,0:T(8,128)S(1)} %get-tuple-element.33.refs_4_.refs_8_), channel_id=1, source_target_pairs={{1,0},{0,1},{3,2},{2,3},{5,4},{4,5},{7,6},{6,7},{9,8},{8,9},{11,10... | collective-permute-start | bytes 122888 | tf_op jit(solution)/shard_map/ppermute | solution.py:581
  22.0 4.1 %collective-permute-start.8 = (f32[10,8,128]{2,1,0:T(8,128)S(1)}, f32[10,8,128]{2,1,0:T(8,128)S(1)}, u32[]{:S(2)}, u32[]{:S(2)}) collective-permute-start(f32[10,8,128]{2,1,0:T(8,128)S(1)} %shard_map.87.refs_4_.refs_10_), channel_id=1, source_target_pairs={{2,0},{3,1},{0,2},{1,3},{6,4},{7,5},{4,6},{5,7},{10,8},{11,9},{8,1... | collective-permute-start | bytes 122888 | tf_op jit(solution)/shard_map/ppermute | solution.py:581
  26.2 8.6 %collective-permute-start.10 = (f32[35,4,128]{2,1,0:T(4,128)S(1)}, f32[35,4,128]{2,1,0:T(4,128)S(1)}, u32[]{:S(2)}, u32[]{:S(2)}) collective-permute-start(f32[35,4,128]{2,1,0:T(4,128)S(1)} %get-tuple-element.35), channel_id=1, source_target_pairs={{6,0},{7,1},{4,2},{5,3},{2,4},{3,5},{0,6},{1,7},{14,8},{15,9},{12,... | collective-permute-start | bytes 215048 | tf_op jit(solution)/shard_map/ppermute | solution.py:581
  28.9 6.0 %collective-permute-start.9 = (f32[25,4,128]{2,1,0:T(4,128)S(1)}, f32[25,4,128]{2,1,0:T(4,128)S(1)}, u32[]{:S(2)}, u32[]{:S(2)}) collective-permute-start(f32[25,4,128]{2,1,0:T(4,128)S(1)} %shard_map.88), channel_id=1, source_target_pairs={{6,0},{7,1},{4,2},{5,3},{2,4},{3,5},{0,6},{1,7},{14,8},{15,9},{12,... | collective-permute-start | bytes 153608 | tf_op jit(solution)/shard_map/ppermute | solution.py:581
